TPU v7x, 256 devices: a whole 4x4x8 slice. The times are simulated.
256 devices in a mesh: ep: 8 (over z), tp: 32 (over y, x, core).
Axes of the slice: x: 4, y: 4, z: 8, core: 2. Of those that a mesh axis runs over, the one named last changes fastest.
Arguments:
- tokens: bfloat16 [768, 3072], P('ep', 'tp'), may hold values from -6 to 6
- cotangent: bfloat16 [768, 3072], P('ep', 'tp'), may hold values from -6 to 6
- expert_ids: int32 [768, 2], P('ep'), may hold values from 0 to 7, all different within a row; in each aligned block of 96 rows (0 to 95, 96 to 191, ...) at most 40 rows name the same one
- combine_weights: float32 [768, 2], P('ep'), may hold values from 0.1 to 1
- w_gate: bfloat16 [8, 3072, 8192], P('ep', None, 'tp'), may hold values from -0.21875 to 0.21875
- w_up: bfloat16 [8, 3072, 8192], P('ep', None, 'tp'), may hold values from -0.109375 to 0.109375
- w_down: bfloat16 [8, 8192, 3072], P('ep', 'tp'), may hold values from -0.125 to 0.125
Outputs:
- mixed: bfloat16 [768, 3072], P('ep', 'tp')
- grad_tokens: bfloat16 [768, 3072], P('ep', 'tp')
- grad_combine: float32 [768, 2], P('ep')
- grad_gate: bfloat16 [8, 3072, 8192], P('ep', 'tp')
- grad_up: bfloat16 [8, 3072, 8192], P('ep', 'tp')
- grad_down: bfloat16 [8, 8192, 3072], P('ep', None, 'tp')
Inputs may be any that keep to these rules, and one draw needn't show every extreme that they name: `expert_ids`: each row names 2 different experts. Among the 96 rows of one index of ep, no expert is named more than 40 times, and in some such blocks one expert is named exactly 40 times.
All inputs are finite; a program needn't handle non-finite values.
Results may differ from a plain program's by a relative error of at most 0.019.
Values may be sent and summed in bfloat16 or wider, within the bound.
A program may use at most 64 MiB of HBM per device.

v0:
```python
import jax
import jax.numpy as jnp
from jax import lax
from jax.sharding import PartitionSpec as P


def in_one_piece(arrays, axis, split_dim, concat_dim, along):
    ends, at = ([], 0)
    for a in arrays[:-1]:
        at += a.shape[along]
        ends.append(at)
    both = jnp.concatenate(arrays, axis=along)
    return tuple(
        jnp.split(
            lax.all_to_all(both, axis, split_axis=split_dim, concat_axis=concat_dim, tiled=True),
            ends,
            axis=along,
        )
    )


def laid_out(pieces, dim):
    pieces = jnp.moveaxis(pieces, 0, dim)
    lengths = pieces.shape
    return pieces.reshape(*lengths[:dim], lengths[dim] * lengths[dim + 1], *lengths[dim + 2 :])


def copy_for_each(x, axis):
    devices = lax.axis_size(axis)
    return lax.all_to_all(jnp.broadcast_to(x[None], (devices, *x.shape)), axis, 0, 0, tiled=True)


def collect(x, axis, dim):
    return laid_out(copy_for_each(x, axis), dim)


def split_up(x, dim, devices):
    lengths = x.shape
    pieces = x.reshape(*lengths[:dim], devices, lengths[dim] // devices, *lengths[dim + 1 :])
    return jnp.moveaxis(pieces, dim, 0)


def sum_at_owner(x, axis, dim):
    devices = lax.axis_size(axis)
    pieces = lax.all_to_all(split_up(x, dim, devices), axis, 0, 0, tiled=True)
    return jnp.sum(pieces.astype(jnp.float32), axis=0)


def over_copies(x, axis):
    return copy_for_each(x, axis).sum(axis=0)


def silu_parts(gate_pre):
    sigma = jax.nn.sigmoid(gate_pre)
    return (gate_pre * sigma, sigma * (1.0 + gate_pre * (1.0 - sigma)))


def contract_rows(left, right):
    return lax.dot_general(
        left, right, (((0,), (0,)), ((), ())), preferred_element_type=jnp.float32
    )


def contract_cols(left, right):
    return lax.dot_general(
        left, right, (((1,), (1,)), ((), ())), preferred_element_type=jnp.float32
    )


def body(tokens, cotangent, expert_ids, combine_weights, w_gate, w_up, w_down):
    groups = lax.axis_size("ep")
    tok_rows, piece_width = tokens.shape
    chosen = expert_ids.shape[1]
    capacity = tok_rows * chosen * 5 // (3 * groups)
    buffer_rows = groups * capacity
    gate_weight = w_gate[0]
    up_weight = w_up[0]
    down_weight = w_down[0]
    hidden_width = gate_weight.shape[1]
    flat_ids = expert_ids.reshape(-1)
    onehot = (flat_ids[:, None] == jnp.arange(groups, dtype=jnp.int32)[None, :]).astype(jnp.int32)
    rank = jnp.sum((jnp.cumsum(onehot, axis=0) - onehot) * onehot, axis=1)
    slot_index = flat_ids * capacity + rank
    places = (jnp.arange(buffer_rows, dtype=jnp.int32)[:, None] == slot_index[None, :]).astype(
        jnp.bfloat16
    )
    placer = jnp.sum(
        places.reshape(buffer_rows, tok_rows, chosen).astype(jnp.float32), axis=2
    ).astype(jnp.bfloat16)
    scaled = (combine_weights[:, :, None] * cotangent[:, None, :].astype(jnp.float32)).astype(
        jnp.bfloat16
    )
    send_grad = jnp.dot(
        places, scaled.reshape(tok_rows * chosen, piece_width), preferred_element_type=jnp.float32
    ).astype(jnp.bfloat16)
    send_rows = jnp.dot(placer, tokens, preferred_element_type=jnp.float32).astype(jnp.bfloat16)
    recv_rows, recv_grad = in_one_piece(
        (
            send_rows.reshape(groups, capacity, piece_width),
            send_grad.reshape(groups, capacity, piece_width),
        ),
        "ep",
        0,
        0,
        1,
    )
    recv_rows = recv_rows.reshape(buffer_rows, piece_width)
    piece = collect(recv_rows, "tp", 1)
    gate_pre = jnp.dot(piece, gate_weight, preferred_element_type=jnp.float32)
    up_pre = jnp.dot(piece, up_weight, preferred_element_type=jnp.float32)
    recv_grad = recv_grad.reshape(buffer_rows, piece_width)
    active, slope = silu_parts(gate_pre)
    hidden = (active * up_pre).astype(jnp.bfloat16)
    partial_value = jnp.dot(hidden, down_weight, preferred_element_type=jnp.float32)
    out_piece = sum_at_owner(partial_value.astype(jnp.bfloat16), "tp", 1).astype(jnp.bfloat16)
    out_back = lax.all_to_all(
        out_piece.reshape(groups, capacity, piece_width),
        "ep",
        split_axis=0,
        concat_axis=0,
        tiled=True,
    ).reshape(buffer_rows, piece_width)
    out_tokens = (
        jnp.take(out_back, slot_index, axis=0)
        .reshape(tok_rows, chosen, piece_width)
        .astype(jnp.float32)
    )
    mixed = jnp.sum(combine_weights[:, :, None] * out_tokens, axis=1).astype(jnp.bfloat16)
    local_products = jnp.sum(cotangent.astype(jnp.float32)[:, None, :] * out_tokens, axis=2)
    grad_combine = over_copies(local_products, "tp")
    grad_hidden = contract_cols(collect(recv_grad, "tp", 1), down_weight)
    down_grad = contract_rows(hidden, collect(recv_grad, "tp", 1))
    grad_gate_pre = (grad_hidden * up_pre * slope).astype(jnp.bfloat16)
    grad_up_pre = (grad_hidden * active).astype(jnp.bfloat16)
    input_partial = contract_cols(grad_gate_pre, gate_weight) + contract_cols(
        grad_up_pre, up_weight
    )
    input_piece = sum_at_owner(input_partial.astype(jnp.bfloat16), "tp", 1).astype(jnp.bfloat16)
    input_back = lax.all_to_all(
        input_piece.reshape(groups, capacity, piece_width),
        "ep",
        split_axis=0,
        concat_axis=0,
        tiled=True,
    ).reshape(buffer_rows, piece_width)
    grad_tokens = jnp.sum(
        jnp.take(input_back, slot_index, axis=0)
        .reshape(tok_rows, chosen, piece_width)
        .astype(jnp.float32),
        axis=1,
    ).astype(jnp.bfloat16)
    stacked = jnp.concatenate([grad_gate_pre, grad_up_pre], axis=1)
    both_grads = contract_rows(collect(recv_rows, "tp", 1), stacked)
    gate_grad = both_grads[:, :hidden_width].astype(jnp.bfloat16)
    up_grad = both_grads[:, hidden_width:].astype(jnp.bfloat16)
    gate_rows_out, up_rows_out = (
        lax.all_to_all(gate_grad, "tp", split_axis=0, concat_axis=1, tiled=True),
        lax.all_to_all(up_grad, "tp", split_axis=0, concat_axis=1, tiled=True),
    )
    down_cols_out = lax.all_to_all(
        down_grad.astype(jnp.bfloat16), "tp", split_axis=1, concat_axis=0, tiled=True
    )
    return (
        mixed,
        grad_tokens,
        grad_combine,
        gate_rows_out[None],
        up_rows_out[None],
        down_cols_out[None],
    )


def solution(mesh):
    placed = (
        P("ep", "tp"),
        P("ep", "tp"),
        P("ep", None),
        P("ep", None),
        P("ep", None, "tp"),
        P("ep", None, "tp"),
        P("ep", "tp", None),
    )
    return jax.shard_map(
        body,
        mesh=mesh,
        in_specs=placed,
        out_specs=(
            P("ep", "tp"),
            P("ep", "tp"),
            P("ep", None),
            P("ep", "tp", None),
            P("ep", "tp", None),
            P("ep", None, "tp"),
        ),
        check_vma=False,
    )
```

profile of v0, /device:TPU:1, one launch (start us, length us, event | category | flops | bytes accessed | tf_op | source)
XLA Modules:
  0.0 327.7 jit_solution(8326589695224463317)
XLA Ops:
  0.6 0.9 copy.105
  2.8 0.8 copy.104
  4.6 0.9 convolution_convert_fusion.3
  5.7 0.8 mul.80
  7.6 17.0 %all_to_all.90 = bf16[8,80,96]{2,1,0:T(8,128)(2,1)S(1)} all-to-all(bf16[8,80,96]{2,1,0:T(8,128)(2,1)S(1)} %pad_maximum_fusion), channel_id=1, replica_groups=mesh['ep'=8,'tp'=32] {'ep'}, dimensions={0} | all-to-all | bytes 245760 | tf_op jit(solution)/shard_map/all_to_all | solution.py:15
  24.7 1.6 broadcast_in_dim.28
  26.3 9.6 %all-to-all-start.1 = ((bf16[32,320,96]{1,2,0:T(8,128)(2,1)}), bf16[32,320,96]{1,2,0:T(8,128)(2,1)}, u32[]{:S(2)}, u32[]{:S(2)}) async-start(bf16[32,320,96]{1,2,0:T(8,128)(2,1)} %broadcast_in_dim.28), calls=%async_computation.1 | async-start | bytes 4718592 | tf_op jit(solution)/shard_map/all_to_all | solution.py:30
  36.1 31.4 %all-to-all-done.1 = bf16[32,320,96]{1,2,0:T(8,128)(2,1)} async-done(((bf16[32,320,96]{1,2,0:T(8,128)(2,1)}), bf16[32,320,96]{1,2,0:T(8,128)(2,1)}, u32[]{:S(2)}, u32[]{:S(2)}) %all-to-all-start.1) | async-done | bytes 1966112 | tf_op jit(solution)/shard_map/all_to_all | solution.py:30
  67.5 1.6 broadcast_in_dim.30
  69.2 6.4 %all-to-all-start.4 = ((bf16[32,320,96]{1,2,0:T(8,128)(2,1)}), bf16[32,320,96]{1,2,0:T(8,128)(2,1)}, u32[]{:S(2)}, u32[]{:S(2)}) async-start(bf16[32,320,96]{1,2,0:T(8,128)(2,1)} %broadcast_in_dim.30), calls=%async_computation.4 | async-start | bytes 4718592 | tf_op jit(solution)/shard_map/all_to_all | solution.py:30
  75.6 2.6 fusion.5
  78.2 2.5 fusion.9
  80.7 26.2 %all-to-all-done.4 = bf16[32,320,96]{1,2,0:T(8,128)(2,1)} async-done(((bf16[32,320,96]{1,2,0:T(8,128)(2,1)}), bf16[32,320,96]{1,2,0:T(8,128)(2,1)}, u32[]{:S(2)}, u32[]{:S(2)}) %all-to-all-start.4) | async-done | bytes 1966112 | tf_op jit(solution)/shard_map/all_to_all | solution.py:30
  106.9 3.4 %multiply_convert_fusion = (bf16[320,256]{1,0:T(8,128)(2,1)}, bf16[320,256]{1,0:T(8,128)(2,1)}, bf16[320,256]{1,0:T(8,128)(2,1)S(1)}) fusion(f32[320,256]{1,0:T(8,128)S(1)} %fusion.9, f32[320,256]{1,0:T(8,128)S(1)} %fusion.5, bf16[320,3072]{0,1:T(8,128)(2,1)} %bitcast.20, bf16[1,256,3072]{2,1,0:T(8,128)(2,1)S(1)} %copy-done), kind=kOutput, calls=%fused_computation.22 | convolution fusion | flops 504545280 | bytes 4685824 | tf_op jit(solution)/shard_map/dot_general | solution.py:65
  110.9 2.7 convolution_convert_fusion.2
  113.7 1.6 copy.119
  115.2 6.0 %all-to-all-start.10 = ((bf16[256,32,96]{0,2,1:T(8,128)(2,1)}), bf16[256,32,96]{0,2,1:T(8,128)(2,1)S(1)}, u32[]{:S(2)}, u32[]{:S(2)}) async-start(bf16[256,32,96]{0,2,1:T(8,128)(2,1)} %bitcast.69), calls=%async_computation.10 | async-start | bytes 3145728 | tf_op jit(solution)/shard_map/all_to_all | solution.py:160
  121.3 3.5 %convolution_convert_fusion = bf16[3072,512]{1,0:T(8,128)(2,1)S(1)} fusion(bf16[320,3072]{0,1:T(8,128)(2,1)} %bitcast.8, bf16[320,256]{1,0:T(8,128)(2,1)S(1)} %copy-done.15, bf16[320,256]{1,0:T(8,128)(2,1)S(1)} %copy-done.13), kind=kOutput, calls=%fused_computation.2 | convolution fusion | flops 1008861184 | bytes 5439488 | tf_op jit(solution)/shard_map/dot_general | solution.py:59
  124.8 1.9 fusion.22
  126.6 17.0 %all-to-all-done.10 = bf16[256,32,96]{0,2,1:T(8,128)(2,1)S(1)} async-done(((bf16[256,32,96]{0,2,1:T(8,128)(2,1)}), bf16[256,32,96]{0,2,1:T(8,128)(2,1)S(1)}, u32[]{:S(2)}, u32[]{:S(2)}) %all-to-all-start.10) | async-done | bytes 1572896 | tf_op jit(solution)/shard_map/all_to_all | solution.py:160
  143.6 29.0 %all_to_all.91 = bf16[32,96,256]{2,1,0:T(8,128)(2,1)} all-to-all(bf16[32,96,256]{2,1,0:T(8,128)(2,1)} %bitcast.71), channel_id=1, replica_groups=mesh['ep'=8,'tp'=32] {'tp'}, dimensions={0} | all-to-all | bytes 3145728 | tf_op jit(solution)/shard_map/all_to_all | solution.py:157
  172.7 4.7 %all-to-all-start.9 = ((bf16[32,96,256]{2,1,0:T(8,128)(2,1)}), bf16[32,96,256]{2,1,0:T(8,128)(2,1)}, u32[]{:S(2)}, u32[]{:S(2)}) async-start(bf16[32,96,256]{2,1,0:T(8,128)(2,1)} %bitcast.70), calls=%async_computation.9 | async-start | bytes 3145728 | tf_op jit(solution)/shard_map/all_to_all | solution.py:158
  177.4 1.6 convolution_convert_fusion.1
  179.0 2.4 copy.111
  181.4 18.3 %all-to-all-done.9 = bf16[32,96,256]{2,1,0:T(8,128)(2,1)} async-done(((bf16[32,96,256]{2,1,0:T(8,128)(2,1)}), bf16[32,96,256]{2,1,0:T(8,128)(2,1)}, u32[]{:S(2)}, u32[]{:S(2)}) %all-to-all-start.9) | async-done | bytes 1572896 | tf_op jit(solution)/shard_map/all_to_all | solution.py:158
  199.7 6.4 %all-to-all-start.2 = ((bf16[32,320,96]{1,2,0:T(8,128)(2,1)}), bf16[32,320,96]{1,2,0:T(8,128)(2,1)}, u32[]{:S(2)}, u32[]{:S(2)}) async-start(bf16[32,320,96]{1,2,0:T(8,128)(2,1)} %bitcast.65), calls=%async_computation.2 | async-start | bytes 4718592 | tf_op jit(solution)/shard_map/all_to_all | solution.py:45
  208.4 2.5 copy.114
  210.8 26.6 %all-to-all-done.2 = bf16[32,320,96]{1,2,0:T(8,128)(2,1)} async-done(((bf16[32,320,96]{1,2,0:T(8,128)(2,1)}), bf16[32,320,96]{1,2,0:T(8,128)(2,1)}, u32[]{:S(2)}, u32[]{:S(2)}) %all-to-all-start.2) | async-done | bytes 1966112 | tf_op jit(solution)/shard_map/all_to_all | solution.py:45
  237.4 6.8 %all-to-all-start.5 = ((bf16[32,320,96]{1,2,0:T(8,128)(2,1)}), bf16[32,320,96]{1,2,0:T(8,128)(2,1)}, u32[]{:S(2)}, u32[]{:S(2)}) async-start(bf16[32,320,96]{1,2,0:T(8,128)(2,1)} %bitcast.66), calls=%async_computation.5 | async-start | bytes 4718592 | tf_op jit(solution)/shard_map/all_to_all | solution.py:45
  244.2 2.2 reduce_sum.89
  246.3 0.7 copy.112
  247.1 28.4 %all-to-all-done.5 = bf16[32,320,96]{1,2,0:T(8,128)(2,1)} async-done(((bf16[32,320,96]{1,2,0:T(8,128)(2,1)}), bf16[32,320,96]{1,2,0:T(8,128)(2,1)}, u32[]{:S(2)}, u32[]{:S(2)}) %all-to-all-start.5) | async-done | bytes 1966112 | tf_op jit(solution)/shard_map/all_to_all | solution.py:45
  275.4 3.4 %all-to-all-start.3 = ((bf16[8,40,96]{2,1,0:T(8,128)(2,1)}), bf16[8,40,96]{2,1,0:T(8,128)(2,1)S(1)}, u32[]{:S(2)}, u32[]{:S(2)}) async-start(bf16[8,40,96]{2,1,0:T(8,128)(2,1)} %bitcast.15), calls=%async_computation.3 | async-start | bytes 163840 | tf_op jit(solution)/shard_map/all_to_all | solution.py:116
  278.8 2.0 copy.120
  280.9 3.9 %broadcast_in_dim.61 = bf16[1,8192,96]{1,2,0:T(8,128)(2,1)} reshape(bf16[32,256,96]{1,0,2:T(8,128)(2,1)} %copy.120) | data formatting | bytes 3145728 | tf_op jit(solution)/shard_map/broadcast_in_dim | solution.py:169
  284.7 2.0 copy.117
  286.7 3.7 %broadcast_in_dim.59 = bf16[1,96,8192]{2,1,0:T(8,128)(2,1)} reshape(bf16[96,32,256]{2,1,0:T(8,128)(2,1)} %copy.117) | data formatting | bytes 3145728 | tf_op jit(solution)/shard_map/broadcast_in_dim | solution.py:167
  290.5 2.3 copy.118
  292.8 2.1 broadcast_in_dim.60
  294.9 2.1 reduce_sum.91
  297.7 6.6 %all-to-all-start.6 = ((bf16[8,40,96]{2,1,0:T(8,128)(2,1)}), bf16[8,40,96]{2,1,0:T(8,128)(2,1)S(1)}, u32[]{:S(2)}, u32[]{:S(2)}) async-start(bf16[8,40,96]{2,1,0:T(8,128)(2,1)} %bitcast.23), calls=%async_computation.6 | async-start | bytes 163840 | tf_op jit(solution)/shard_map/all_to_all | solution.py:139
  304.2 0.8 gather_fusion
  305.4 6.3 %all-to-all-done.6 = bf16[8,40,96]{2,1,0:T(8,128)(2,1)S(1)} async-done(((bf16[8,40,96]{2,1,0:T(8,128)(2,1)}), bf16[8,40,96]{2,1,0:T(8,128)(2,1)S(1)}, u32[]{:S(2)}, u32[]{:S(2)}) %all-to-all-start.6) | async-done | bytes 61472 | tf_op jit(solution)/shard_map/all_to_all | solution.py:139
  312.4 7.4 %all-to-all-start.7 = ((f32[32,96,2]{1,2,0:T(2,128)}), f32[32,96,2]{1,2,0:T(2,128)S(1)}, u32[]{:S(2)}, u32[]{:S(2)}) async-start(f32[32,96,2]{1,2,0:T(2,128)} %broadcast_in_dim.58), calls=%async_computation.7 | async-start | bytes 65536 | tf_op jit(solution)/shard_map/all_to_all | solution.py:30
  319.7 0.8 gather_fusion.1
  320.6 0.8 multiply_reduce_fusion.1
  321.5 0.7 reduce_sum.92
  322.2 4.9 %all-to-all-done.7 = f32[32,96,2]{1,2,0:T(2,128)S(1)} async-done(((f32[32,96,2]{1,2,0:T(2,128)}), f32[32,96,2]{1,2,0:T(2,128)S(1)}, u32[]{:S(2)}, u32[]{:S(2)}) %all-to-all-start.7) | async-done | bytes 24608 | tf_op jit(solution)/shard_map/all_to_all | solution.py:30
  (68 shorter events, 9.0 us)
Async XLA Ops:
  0.6 106.3 %copy-start = (bf16[1,256,3072]{2,1,0:T(8,128)(2,1)S(1)}, bf16[1,256,3072]{2,1,0:T(8,128)(2,1)}, u32[]{:S(2)}) copy-start(bf16[1,256,3072]{2,1,0:T(8,128)(2,1)} %param.15) | copy-start | bytes 4718596
  3.6 22.7 %copy-start.11 = (f32[96,2]{1,0:T(8,128)}, f32[96,2]{1,0:T(8,128)S(1)}, u32[]{:S(2)}) copy-start(f32[96,2]{1,0:T(8,128)S(1)} %copy.104) | copy-start | bytes 2308
  6.5 0.6 copy-start.9
  26.3 41.2 %all-to-all-start.1 = ((bf16[32,320,96]{1,2,0:T(8,128)(2,1)}), bf16[32,320,96]{1,2,0:T(8,128)(2,1)}, u32[]{:S(2)}, u32[]{:S(2)}) async-start(bf16[32,320,96]{1,2,0:T(8,128)(2,1)} %broadcast_in_dim.28), calls=%async_computation.1 | async-start | bytes 4718592 | tf_op jit(solution)/shard_map/all_to_all | solution.py:30
  69.2 6.4 %copy-start.6 = (bf16[1,3072,256]{2,1,0:T(8,128)(2,1)S(1)}, bf16[1,3072,256]{2,1,0:T(8,128)(2,1)}, u32[]{:S(2)}) copy-start(bf16[1,3072,256]{2,1,0:T(8,128)(2,1)} %param.14) | copy-start | bytes 4718596
  69.2 37.7 %all-to-all-start.4 = ((bf16[32,320,96]{1,2,0:T(8,128)(2,1)}), bf16[32,320,96]{1,2,0:T(8,128)(2,1)}, u32[]{:S(2)}, u32[]{:S(2)}) async-start(bf16[32,320,96]{1,2,0:T(8,128)(2,1)} %broadcast_in_dim.30), calls=%async_computation.4 | async-start | bytes 4718592 | tf_op jit(solution)/shard_map/all_to_all | solution.py:30
  75.6 2.6 copy-start.4
  110.3 0.7 copy-start.8
  115.2 6.1 %copy-start.13 = (bf16[320,256]{1,0:T(8,128)(2,1)S(1)}, bf16[320,256]{1,0:T(8,128)(2,1)}, u32[]{:S(2)}) copy-start(bf16[320,256]{1,0:T(8,128)(2,1)} %get-tuple-element.12) | copy-start | bytes 491524
  115.2 6.1 %copy-start.15 = (bf16[320,256]{1,0:T(8,128)(2,1)S(1)}, bf16[320,256]{1,0:T(8,128)(2,1)}, u32[]{:S(2)}) copy-start(bf16[320,256]{1,0:T(8,128)(2,1)} %get-tuple-element.11) | copy-start | bytes 491524
  115.2 28.4 %all-to-all-start.10 = ((bf16[256,32,96]{0,2,1:T(8,128)(2,1)}), bf16[256,32,96]{0,2,1:T(8,128)(2,1)S(1)}, u32[]{:S(2)}, u32[]{:S(2)}) async-start(bf16[256,32,96]{0,2,1:T(8,128)(2,1)} %bitcast.69), calls=%async_computation.10 | async-start | bytes 3145728 | tf_op jit(solution)/shard_map/all_to_all | solution.py:160
  143.6 29.0 %copy-start.1 = (bf16[256,32,96]{0,2,1:T(8,128)(2,1)}, bf16[256,32,96]{0,2,1:T(8,128)(2,1)S(1)}, u32[]{:S(2)}) copy-start(bf16[256,32,96]{0,2,1:T(8,128)(2,1)S(1)} %all-to-all-done.10) | copy-start | bytes 4718596
  172.7 27.1 %all-to-all-start.9 = ((bf16[32,96,256]{2,1,0:T(8,128)(2,1)}), bf16[32,96,256]{2,1,0:T(8,128)(2,1)}, u32[]{:S(2)}, u32[]{:S(2)}) async-start(bf16[32,96,256]{2,1,0:T(8,128)(2,1)} %bitcast.70), calls=%async_computation.9 | async-start | bytes 3145728 | tf_op jit(solution)/shard_map/all_to_all | solution.py:158
  199.7 6.5 %copy-start.5 = (bf16[1,3072,256]{2,1,0:T(8,128)(2,1)S(1)}, bf16[1,3072,256]{2,1,0:T(8,128)(2,1)}, u32[]{:S(2)}) copy-start(bf16[1,3072,256]{2,1,0:T(8,128)(2,1)} %param.13) | copy-start | bytes 4718596
  199.7 6.5 %copy-start.14 = (bf16[320,256]{1,0:T(8,128)(2,1)S(1)}, bf16[320,256]{1,0:T(8,128)(2,1)}, u32[]{:S(2)}) copy-start(bf16[320,256]{1,0:T(8,128)(2,1)} %get-tuple-element.12) | copy-start | bytes 491524
  199.7 37.6 %all-to-all-start.2 = ((bf16[32,320,96]{1,2,0:T(8,128)(2,1)}), bf16[32,320,96]{1,2,0:T(8,128)(2,1)}, u32[]{:S(2)}, u32[]{:S(2)}) async-start(bf16[32,320,96]{1,2,0:T(8,128)(2,1)} %bitcast.65), calls=%async_computation.2 | async-start | bytes 4718592 | tf_op jit(solution)/shard_map/all_to_all | solution.py:45
  206.2 1.4 copy-start.7
  206.2 1.4 copy-start.16
  237.4 38.1 %all-to-all-start.5 = ((bf16[32,320,96]{1,2,0:T(8,128)(2,1)}), bf16[32,320,96]{1,2,0:T(8,128)(2,1)}, u32[]{:S(2)}, u32[]{:S(2)}) async-start(bf16[32,320,96]{1,2,0:T(8,128)(2,1)} %bitcast.66), calls=%async_computation.5 | async-start | bytes 4718592 | tf_op jit(solution)/shard_map/all_to_all | solution.py:45
  244.2 34.7 %copy-start.2 = (bf16[256,32,96]{0,2,1:T(8,128)(2,1)S(1)}, bf16[256,32,96]{0,2,1:T(8,128)(2,1)}, u32[]{:S(2)}) copy-start(bf16[256,32,96]{0,2,1:T(8,128)(2,1)} %copy-done.1) | copy-start | bytes 4718596
  275.4 22.2 %all-to-all-start.3 = ((bf16[8,40,96]{2,1,0:T(8,128)(2,1)}), bf16[8,40,96]{2,1,0:T(8,128)(2,1)S(1)}, u32[]{:S(2)}, u32[]{:S(2)}) async-start(bf16[8,40,96]{2,1,0:T(8,128)(2,1)} %bitcast.15), calls=%async_computation.3 | async-start | bytes 163840 | tf_op jit(solution)/shard_map/all_to_all | solution.py:116
  280.9 3.9 %copy-start.3 = (bf16[32,96,256]{2,1,0:T(8,128)(2,1)S(1)}, bf16[32,96,256]{2,1,0:T(8,128)(2,1)}, u32[]{:S(2)}) copy-start(bf16[32,96,256]{2,1,0:T(8,128)(2,1)} %all_to_all.91) | copy-start | bytes 4718596
  294.9 10.2 %copy-start.10 = (f32[96,2,96]{2,1,0:T(2,128)S(1)}, f32[96,2,96]{2,1,0:T(2,128)}, u32[]{:S(2)}) copy-start(f32[96,2,96]{2,1,0:T(2,128)} %copy-done.9) | copy-start | bytes 221188
  294.9 25.8 %copy-start.12 = (f32[96,2]{1,0:T(8,128)S(1)}, f32[96,2]{1,0:T(8,128)}, u32[]{:S(2)}) copy-start(f32[96,2]{1,0:T(8,128)} %copy-done.11) | copy-start | bytes 2308
  297.7 14.1 %all-to-all-start.6 = ((bf16[8,40,96]{2,1,0:T(8,128)(2,1)}), bf16[8,40,96]{2,1,0:T(8,128)(2,1)S(1)}, u32[]{:S(2)}, u32[]{:S(2)}) async-start(bf16[8,40,96]{2,1,0:T(8,128)(2,1)} %bitcast.23), calls=%async_computation.6 | async-start | bytes 163840 | tf_op jit(solution)/shard_map/all_to_all | solution.py:139
  312.4 14.7 %all-to-all-start.7 = ((f32[32,96,2]{1,2,0:T(2,128)}), f32[32,96,2]{1,2,0:T(2,128)S(1)}, u32[]{:S(2)}, u32[]{:S(2)}) async-start(f32[32,96,2]{1,2,0:T(2,128)} %broadcast_in_dim.58), calls=%async_computation.7 | async-start | bytes 65536 | tf_op jit(solution)/shard_map/all_to_all | solution.py:30
where the time goes:
time: 329 us; the launch traced here: 328 us
  waiting for transfers between devices  159 us (48%)
  starting transfers between devices  57.3 us (17%)
  blocking collectives  46 us (14%)
  local copies, waits for them, and re-layouts  37.1 us (11%)
  matrix products  18.8 us (6%)
  other arithmetic  8.29 us (3%)
    all_to_all x3, waiting for transfers between devices, copy_for_each(): lax.all_to_all(jnp.broadcast_to(x[None], (devices, *x.shape)), axis, 0, 0...  62.5 us
    all_to_all x2, waiting for transfers between devices, sum_at_owner(): pieces = lax.all_to_all(split_up(x, dim, devices), axis, 0, 0, tiled=True)  54.9 us
    all_to_all x1, blocking collectives, body(): lax.all_to_all(gate_grad, 'tp', split_axis=0, concat_axis=1, tiled=True)  29 us
    all_to_all x3, starting transfers between devices, copy_for_each(): lax.all_to_all(jnp.broadcast_to(x[None], (devices, *x.shape)), axis, 0, 0...  23.4 us
    all_to_all x1, waiting for transfers between devices, body(): lax.all_to_all(up_grad, 'tp', split_axis=0, concat_axis=1, tiled=True)  18.3 us
    all_to_all x1, blocking collectives, in_one_piece(): lax.all_to_all(both, axis, split_axis=split_dim, concat_axis=concat_dim,...  17 us
    all_to_all x1, waiting for transfers between devices, body(): lax.all_to_all(down_grad.astype(jnp.bfloat16), 'tp', split_axis=1, concat...  17 us
    all_to_all x2, starting transfers between devices, sum_at_owner(): pieces = lax.all_to_all(split_up(x, dim, devices), axis, 0, 0, tiled=True)  13.2 us
  transfers between devices with their start and end apart: 9, of which 8 were waited for; matrix products, arithmetic and copies ran while one was open for 13% of the time, Pallas kernels for 0%

commit v1 on v0

v1 whole, which is shorter than its diff:
```python
import functools

import jax
import jax.numpy as jnp
from jax import lax
from jax.experimental import pallas as pl
from jax.experimental.pallas import tpu as pltpu
from jax.sharding import PartitionSpec as P

SIDE = 4
CAP = 40
HALF = 48
PAIR = 2 * HALF
GROUPS = 8
ROWS = GROUPS * PAIR
SLOTS = GROUPS * CAP
PACK = 2 * SLOTS
WIN = 384
F32 = jnp.float32
BF16 = jnp.bfloat16
VMEM = pl.BlockSpec(memory_space=pltpu.VMEM)


def dot(a, b, ca, cb):
    return lax.dot_general(a, b, (((ca,), (cb,)), ((), ())), preferred_element_type=F32)


def iota(shape, dim):
    return lax.broadcasted_iota(jnp.int32, shape, dim)


class Grid:
    def __init__(self):
        t = lax.axis_index("tp")
        self.tp = t
        self.c = t % 2
        self.x = (t // 2) % SIDE
        self.y = t // (2 * SIDE)
        self.z = lax.axis_index("ep")

    def at(self, dy, dx, other=False):
        y = (self.y + (dy + SIDE)) % SIDE
        x = (self.x + (dx + SIDE)) % SIDE
        c = 1 - self.c if other else self.c
        return (y * SIDE + x) * 2 + c

    def block(self, h, o1, o2, other=False):
        return self.at(o2, o1, other) if h == 0 else self.at(o1, o2, other)

    def up(self, k):
        return (self.z + k) % GROUPS


class Copies:
    def __init__(self, send, recv):
        self.send, self.recv, self.n, self.ids, self.started = send, recv, 0, {}, []

    def make(self, key, src, dst, to):
        if key not in self.ids:
            self.ids[key] = len(self.ids)
        j = self.ids[key]
        return pltpu.make_async_remote_copy(
            src_ref=src,
            dst_ref=dst,
            send_sem=self.send.at[j],
            recv_sem=self.recv.at[j],
            device_id=to,
            device_id_type=pl.DeviceIdType.MESH,
        )

    def start(self, key, src, dst, to):
        c = self.make(key, src, dst, to)
        c.start()
        self.started.append(c)

    def wait(self, key, dst, to):
        self.make(key, dst, dst, to).wait_recv()

    def finish(self):
        for c in self.started:
            c.wait_send()


def greet(partners):
    barrier = pltpu.get_barrier_semaphore()
    for to in partners:
        pl.semaphore_signal(barrier, inc=1, device_id=to, device_id_type=pl.DeviceIdType.MESH)
    pl.semaphore_wait(barrier, len(partners))


def gather(g, cp, half, part, tick):
    sib = {"tp": g.at(0, 0, True)}

    def nbr(h, axis, d):
        return {"tp": g.block(h, d, 0) if axis == 1 else g.block(h, 0, d)}

    def send(key, h, axis, d, ref):
        cp.start(key, ref, ref, nbr(h, axis, d))

    def got(key, h, axis, d, ref):
        cp.wait(key, ref, nbr(h, axis, d))

    def across(h, o1, o2):
        ref = half(g.block(h, o1, o2), h)
        cp.start(("s", h, o1, o2), ref, ref, sib)

    def from_sib(h, o1, o2):
        b = g.block(h, o1, o2, True)
        cp.wait(("s", h, o1, o2), half(b, h), sib)
        tick(b, h)

    dirs = (1, -1)
    for h in (0, 1):
        for d in dirs:
            send(("p1", h, d), h, 1, d, half(g.tp, h))
    for h in (0, 1):
        for d in dirs:
            send(("p2", h, 0, d), h, 2, d, half(g.tp, h))
    for h in (0, 1):
        across(h, 0, 0)
    yield
    for h in (0, 1):
        tick(g.tp, h)
        from_sib(h, 0, 0)
    for d in dirs:
        for h in (0, 1):
            b = g.block(h, -d, 0)
            got(("p1", h, d), h, 1, -d, half(b, h))
            send(("f1", h, d), h, 1, d, part(b, h, d, 0))
            for e in dirs:
                send(("p2", h, -d, e), h, 2, e, half(b, h))
            across(h, -d, 0)
            tick(b, h)
    yield
    for e in dirs:
        for h in (0, 1):
            b = g.block(h, 0, -e)
            got(("p2", h, 0, e), h, 2, -e, half(b, h))
            send(("f2", h, 0, e), h, 2, e, part(b, h, e, 0))
            across(h, 0, -e)
            tick(b, h)
            from_sib(h, -e, 0)
    yield
    for h in (0, 1):
        b = g.block(h, 2, 0)
        for d in dirs:
            got(("f1", h, d), h, 1, -d, part(b, h, d, 0))
        for e in dirs:
            send(("p2", h, 2, e), h, 2, e, half(b, h))
        across(h, 2, 0)
        tick(b, h)
        from_sib(h, 0, -1)
        from_sib(h, 0, 1)
    yield
    for o1 in (-1, 1):
        for e in dirs:
            for h in (0, 1):
                b = g.block(h, o1, -e)
                got(("p2", h, o1, e), h, 2, -e, half(b, h))
                send(("f2", h, o1, e), h, 2, e, part(b, h, e, o1))
                across(h, o1, -e)
                tick(b, h)
                if (o1, e) == (-1, 1):
                    from_sib(h, 2, 0)
    yield
    for h in (0, 1):
        b = g.block(h, 0, 2)
        for e in dirs:
            got(("f2", h, 0, e), h, 2, -e, part(b, h, e, 0))
        across(h, 0, 2)
        tick(b, h)
        for o1 in (-1, 1):
            for e in dirs:
                from_sib(h, o1, -e)
    yield
    for e in dirs:
        for h in (0, 1):
            b = g.block(h, 2, -e)
            got(("p2", h, 2, e), h, 2, -e, half(b, h))
            send(("f2", h, 2, e), h, 2, e, part(b, h, e, 2))
            across(h, 2, -e)
            tick(b, h)
            if e == 1:
                from_sib(h, 0, 2)
    yield
    for o1 in (-1, 1):
        for h in (0, 1):
            b = g.block(h, o1, 2)
            for e in dirs:
                got(("f2", h, o1, e), h, 2, -e, part(b, h, e, o1))
            across(h, o1, 2)
            tick(b, h)
            from_sib(h, 2, -o1)
    yield
    for h in (0, 1):
        b = g.block(h, 2, 2)
        for e in dirs:
            got(("f2", h, 2, e), h, 2, -e, part(b, h, e, 2))
        across(h, 2, 2)
        tick(b, h)
        from_sib(h, -1, 2)
        from_sib(h, 1, 2)
    for h in (0, 1):
        from_sib(h, 2, 2)
    yield


def places(ids):
    n = ids.shape[0]
    lane = iota((n, 128), 1)
    before = (iota((n, n), 1) < iota((n, n), 0)).astype(BF16)
    hot = [(ids[:, k : k + 1] == lane).astype(F32) for k in (0, 1)]
    seen = [dot(before, hot[k].astype(BF16), 1, 0) for k in (0, 1)]
    seen[1] = seen[1] + jnp.sum(hot[0], axis=0, keepdims=True)
    rank = [jnp.sum(seen[k] * hot[k], axis=1, keepdims=True) for k in (0, 1)]
    row = [ids[:, k : k + 1].astype(F32) * PAIR + rank[k] for k in (0, 1)]
    lanes = iota((n, ROWS), 1).astype(F32)
    first = [(lanes == row[k]).astype(BF16) for k in (0, 1)]
    second = [(lanes == row[k] + HALF).astype(BF16) for k in (0, 1)]
    return first, second


def packing():
    r = iota((ROWS, PACK), 0)
    lane = iota((ROWS, PACK), 1)
    j = r % PAIR
    grad = j >= HALF
    k = jnp.where(grad, j - HALF, j)
    s = (r // PAIR) * CAP + k
    want = jnp.where(grad, jnp.where(s < 256, s + 384, s + 64), s)
    return ((want == lane) & (k < CAP)).astype(BF16)


def to_all_groups(g, cp, src, dst, name):
    for k in range(1, GROUPS):
        to = g.up(k)
        cp.start(
            (name, k),
            src.at[pl.ds(pl.multiple_of(to * PAIR, PAIR), PAIR)],
            dst.at[pl.ds(pl.multiple_of(g.z * PAIR, PAIR), PAIR)],
            {"ep": to},
        )


def from_all_groups(g, cp, dst, name):
    for k in range(1, GROUPS):
        frm = g.up(GROUPS - k)
        cp.wait((name, k), dst.at[pl.ds(pl.multiple_of(frm * PAIR, PAIR), PAIR)], {"ep": frm})


def own_group(g, src, dst):
    mine = pl.ds(pl.multiple_of(g.z * PAIR, PAIR), PAIR)
    dst[mine] = src[mine]


def dispatch_kernel(tok_ref, cot_ref, ids_ref, w_ref, own_ref, all_ref, rows, got, send, recv):
    g = Grid()
    cp = Copies(send, recv)
    greet(
        [{"tp": g.at(0, 0, True)}]
        + [{"tp": g.at(*o)} for o in ((0, 1), (0, -1), (1, 0), (-1, 0))]
        + [{"ep": g.up(k)} for k in range(1, GROUPS)]
    )
    first, second = places(ids_ref[...])
    cot = cot_ref[...].astype(F32)
    w = w_ref[...]
    scaled = [(w[:, k : k + 1] * cot).astype(BF16) for k in (0, 1)]
    sent = dot(first[0] + first[1], tok_ref[...], 0, 0)
    sent = sent + dot(second[0], scaled[0], 0, 0) + dot(second[1], scaled[1], 0, 0)
    rows[...] = sent.astype(BF16)
    to_all_groups(g, cp, rows, got, "out")
    own_group(g, rows, got)
    pack = packing()
    from_all_groups(g, cp, got, "out")
    own = dot(got[...], pack, 0, 0).astype(BF16)
    own_ref[...] = own
    size = own.shape[0]
    all_ref[pl.ds(pl.multiple_of(g.tp * size, size), size), :] = own
    hh = size // 2

    def half(b, h):
        return all_ref.at[pl.ds(pl.multiple_of(b * size + h * hh, 16), hh)]

    def part(b, h, q, o):
        low = (q > 0) == (o in (0, 1))
        rng = pl.ds(0, 384) if low else pl.ds(384, 256)
        return all_ref.at[pl.ds(pl.multiple_of(b * size + h * hh, 16), hh), rng]

    for _ in gather(g, cp, half, part, lambda b, h: None):
        pass
    cp.finish()


N_DISPATCH = 7 + 40 + 32


def dispatch(tokens, cotangent, ids, weights):
    width = tokens.shape[1]
    return pl.pallas_call(
        dispatch_kernel,
        out_shape=(
            jax.ShapeDtypeStruct((width, PACK), BF16),
            jax.ShapeDtypeStruct((2 * SIDE * SIDE * width, PACK), BF16),
        ),
        in_specs=[VMEM] * 4,
        out_specs=(VMEM, VMEM),
        scratch_shapes=[
            pltpu.VMEM((ROWS, width), BF16),
            pltpu.VMEM((ROWS, width), BF16),
            pltpu.SemaphoreType.DMA((N_DISPATCH,)),
            pltpu.SemaphoreType.DMA((N_DISPATCH,)),
        ],
        compiler_params=pltpu.CompilerParams(
            collective_id=0, has_side_effects=True, vmem_limit_bytes=60 * 2**20
        ),
        name="dispatch",
    )(tokens, cotangent, ids, weights)


def back_kernel(
    part_ref, act_ref, xg_ref, xu_ref, dy_ref, cot_ref, ids_ref, w_ref,
    gate_ref, up_ref, down_ref, mixed_ref, gt_ref, gc_ref,
    full, sib, chip, ra, rb, mid, fin, rows, got, red, send, recv,
):
    g = Grid()
    cp = Copies(send, recv)
    ring = ((0, 1), (0, -1), (0, 2), (1, 0), (-1, 0), (2, 0))
    greet(
        [{"tp": g.at(0, 0, True)}]
        + [{"tp": g.at(*o)} for o in ring]
        + [{"ep": g.up(k)} for k in range(1, GROUPS)]
    )
    size = act_ref.shape[0]
    hh = size // 2
    width = part_ref.shape[2]
    half_w = width // 2
    sib_dev = {"tp": g.at(0, 0, True)}

    def half(b, h):
        return full.at[pl.ds(pl.multiple_of(b * size + h * hh, 64), hh)]

    def part(b, h, q, o):
        off = 0 if q > 0 else hh // 2
        return full.at[pl.ds(pl.multiple_of(b * size + h * hh + off, 64), hh // 2)]

    def tick(b, h):
        at = pl.multiple_of(b * size + h * hh, 128)
        blk = full[pl.ds(at, hh), :]
        down_ref[pl.ds(at, hh), :] = dot(blk[:, :WIN], dy_ref[...], 1, 0).astype(BF16)
        gate_ref[:, pl.ds(at, hh)] = dot(xg_ref[...], blk[:, 256:640], 1, 1).astype(BF16)
        up_ref[:, pl.ds(at, hh)] = dot(xu_ref[...], blk[:, 640:], 1, 1).astype(BF16)

    cp.start("pair", part_ref.at[:, 1 - g.c], sib, sib_dev)
    mine = pl.ds(pl.multiple_of(g.tp * size, 256), size)
    full[mine, :] = act_ref[...]
    cp.wait("pair", sib, sib_dev)

    def add_pair(i, _):
        chip[i] = (part_ref[i, g.c].astype(F32) + sib[i].astype(F32)).astype(BF16)
        return _

    lax.fori_loop(0, SIDE * SIDE, add_pair, 0)

    def y_of(d):
        return (g.y + d + SIDE) % SIDE

    def x_of(d):
        return (g.x + d + SIDE) % SIDE

    lo, hi = pl.ds(0, half_w), pl.ds(half_w, half_w)
    for i, d in enumerate((1, -1, 2)):
        cp.start(("a1", d), chip.at[pl.ds(y_of(d) * SIDE, SIDE), lo], ra.at[i], {"tp": g.at(d, 0)})
        for r in range(SIDE):
            cp.start(("b1", d, r), chip.at[r * SIDE + x_of(d), hi], rb.at[i, r], {"tp": g.at(0, d)})
    steps = gather(g, cp, half, part, tick)
    next(steps)
    for i, d in enumerate((1, -1, 2)):
        cp.wait(("a1", d), ra.at[i], {"tp": g.at(-d, 0)})
        for r in range(SIDE):
            cp.wait(("b1", d, r), rb.at[i, r], {"tp": g.at(0, -d)})

    def add_a(r, _):
        s = chip[g.y * SIDE + r, lo, :].astype(F32)
        for i in range(3):
            s = s + ra[i, r].astype(F32)
        mid[0, r] = s.astype(BF16)
        s = chip[r * SIDE + g.x, hi, :].astype(F32)
        for i in range(3):
            s = s + rb[i, r].astype(F32)
        mid[1, r] = s.astype(BF16)
        return _

    lax.fori_loop(0, SIDE, add_a, 0)
    for i, d in enumerate((1, -1, 2)):
        cp.start(("a2", d), mid.at[0, x_of(d)], fin.at[0, i], {"tp": g.at(0, d)})
        cp.start(("b2", d), mid.at[1, y_of(d)], fin.at[1, i], {"tp": g.at(d, 0)})
    next(steps)
    next(steps)
    for i, d in enumerate((1, -1, 2)):
        cp.wait(("a2", d), fin.at[0, i], {"tp": g.at(0, -d)})
        cp.wait(("b2", d), fin.at[1, i], {"tp": g.at(-d, 0)})
    sums = []
    for h in (0, 1):
        s = mid[h, g.x if h == 0 else g.y].astype(F32)
        for i in range(3):
            s = s + fin[h, i].astype(F32)
        sums.append(s)
    own = jnp.concatenate(sums, axis=0).astype(BF16)
    rows[...] = dot(packing(), own, 1, 1).astype(BF16)
    to_all_groups(g, cp, rows, got, "back")
    own_group(g, rows, got)
    next(steps)
    first, second = places(ids_ref[...])
    from_all_groups(g, cp, got, "back")
    back = got[...]
    cot = cot_ref[...].astype(F32)
    w = w_ref[...]
    outs = [dot(first[k], back, 1, 0) for k in (0, 1)]
    mixed_ref[...] = (w[:, 0:1] * outs[0] + w[:, 1:2] * outs[1]).astype(BF16)
    gt_ref[...] = (dot(second[0], back, 1, 0) + dot(second[1], back, 1, 0)).astype(BF16)
    inner = [jnp.sum(cot * outs[k], axis=1, keepdims=True) for k in (0, 1)]
    lane = iota((inner[0].shape[0], 128), 1)
    red[0] = jnp.where(lane == 0, inner[0], jnp.where(lane == 1, inner[1], 0.0))
    cp.start("g0", red.at[0], red.at[1], sib_dev)
    next(steps)
    cp.wait("g0", red.at[1], sib_dev)
    red[2 + g.x] = red[0] + red[1]
    for d in (1, -1, 2):
        cp.start(("g1", d), red.at[2 + g.x], red.at[2 + g.x], {"tp": g.at(0, d)})
    next(steps)
    for d in (1, -1, 2):
        cp.wait(("g1", d), red.at[2 + x_of(-d)], {"tp": g.at(0, -d)})
    red[6 + g.y] = (red[2] + red[3]) + (red[4] + red[5])
    for d in (1, -1, 2):
        cp.start(("g2", d), red.at[6 + g.y], red.at[6 + g.y], {"tp": g.at(d, 0)})
    for _ in steps:
        pass
    for d in (1, -1, 2):
        cp.wait(("g2", d), red.at[6 + y_of(-d)], {"tp": g.at(-d, 0)})
    gc_ref[...] = ((red[6] + red[7]) + (red[8] + red[9]))[:, :2]
    cp.finish()


N_BACK = 1 + 15 + 72 + 6 + 7 + 7


def back(part, act, xg, xu, dy, cotangent, ids, weights):
    width = cotangent.shape[1]
    size = act.shape[0]
    n = 2 * SIDE * SIDE
    return pl.pallas_call(
        back_kernel,
        out_shape=(
            jax.ShapeDtypeStruct((width, n * size), BF16),
            jax.ShapeDtypeStruct((width, n * size), BF16),
            jax.ShapeDtypeStruct((n * size, width), BF16),
            jax.ShapeDtypeStruct(cotangent.shape, BF16),
            jax.ShapeDtypeStruct(cotangent.shape, BF16),
            jax.ShapeDtypeStruct(ids.shape, F32),
        ),
        in_specs=[VMEM] * 8,
        out_specs=(VMEM,) * 6,
        scratch_shapes=[
            pltpu.VMEM((n * size, act.shape[1]), BF16),
            pltpu.VMEM((SIDE * SIDE, width, PACK), BF16),
            pltpu.VMEM((SIDE * SIDE, width, PACK), BF16),
            pltpu.VMEM((3, SIDE, width // 2, PACK), BF16),
            pltpu.VMEM((3, SIDE, width // 2, PACK), BF16),
            pltpu.VMEM((2, SIDE, width // 2, PACK), BF16),
            pltpu.VMEM((2, 3, width // 2, PACK), BF16),
            pltpu.VMEM((ROWS, width), BF16),
            pltpu.VMEM((ROWS, width), BF16),
            pltpu.VMEM((10, width, 128), F32),
            pltpu.SemaphoreType.DMA((N_BACK,)),
            pltpu.SemaphoreType.DMA((N_BACK,)),
        ],
        compiler_params=pltpu.CompilerParams(
            collective_id=1, has_side_effects=True, vmem_limit_bytes=60 * 2**20
        ),
        name="back",
    )(part, act, xg, xu, dy, cotangent, ids, weights)


def body(tokens, cotangent, expert_ids, combine_weights, w_gate, w_up, w_down):
    width = tokens.shape[1]
    gate_w, up_w, down_w = w_gate[0], w_up[0], w_down[0]
    own, xd = dispatch(tokens, cotangent, expert_ids, combine_weights)
    gate_pre = dot(gate_w, xd[:, :WIN], 0, 0)
    up_pre = dot(up_w, xd[:, :WIN], 0, 0)
    gh = dot(down_w, xd[:, 256:], 1, 0)
    gh = jnp.concatenate([gh[:, 128:], gh[:, 64:128], gh[:, 0:64]], axis=1)
    live = iota(gh.shape, 1) < SLOTS
    sigma = jax.nn.sigmoid(gate_pre)
    active = gate_pre * sigma
    slope = sigma * (1.0 + gate_pre * (1.0 - sigma))
    hidden = jnp.where(live, active * up_pre, 0.0).astype(BF16)
    ggp = jnp.where(live, gh * up_pre * slope, 0.0).astype(BF16)
    gup = jnp.where(live, gh * active, 0.0).astype(BF16)
    act = jnp.concatenate([hidden[:, :SLOTS], ggp[:, 256:SLOTS], ggp[:, :256], gup], axis=1)
    out = dot(down_w, hidden[:, :SLOTS], 0, 0).astype(BF16)
    grad = (dot(gate_w, ggp[:, :SLOTS], 1, 0) + dot(up_w, gup[:, :SLOTS], 1, 0)).astype(BF16)
    part = jnp.concatenate([out, grad[:, 256:], grad[:, :256]], axis=1)
    part = part.reshape(SIDE * SIDE, 2, width, PACK)
    zero = jnp.zeros((width, 64), BF16)
    xg = jnp.concatenate([zero, own[:, 256:320], own[:, :256]], axis=1)
    xu = jnp.concatenate([own[:, :320], zero], axis=1)
    dy = jnp.concatenate([own[:, 384:], own[:, 320:384], zero], axis=1).T
    gate, up, down, mixed, gt, gc = back(
        part, act, xg, xu, dy, cotangent, expert_ids, combine_weights
    )
    return mixed, gt, gc, gate[None], up[None], down[None]


def solution(mesh):
    placed = (
        P("ep", "tp"),
        P("ep", "tp"),
        P("ep", None),
        P("ep", None),
        P("ep", None, "tp"),
        P("ep", None, "tp"),
        P("ep", "tp", None),
    )
    return jax.shard_map(
        body,
        mesh=mesh,
        in_specs=placed,
        out_specs=(
            P("ep", "tp"),
            P("ep", "tp"),
            P("ep", None),
            P("ep", "tp", None),
            P("ep", "tp", None),
            P("ep", None, "tp"),
        ),
        check_vma=False,
    )
```

time: 329 us -> 159 us (0.48)
  waiting for transfers between devices: 159 us -> 0 us
  Pallas kernels: 0 us -> 122 us
  starting transfers between devices: 57.3 us -> 0 us
  blocking collectives: 46 us -> 0 us
  local copies, waits for them, and re-layouts: 37.1 us -> 21.9 us
  matrix products: 18.8 us -> 8.13 us
    all_to_all x9 -> x0, waiting for transfers between devices: 159 us -> none  [the longest x3 62.5 us: copy_for_each(): lax.all_to_all(jnp.broadcast_to(x[None], (devices, *x.shape)), axis, 0, 0...]
    pallas_call x0 -> x2, Pallas kernels: none -> 122 us  [the longest x1 82.9 us: back(): pl.pallas_call(back_kernel, out_shape=(jax.ShapeDtypeStruct((width, n * s...]
    all_to_all x9 -> x0, starting transfers between devices: 57.3 us -> none  [the longest x3 23.4 us: copy_for_each(): lax.all_to_all(jnp.broadcast_to(x[None], (devices, *x.shape)), axis, 0, 0...]
    all_to_all x2 -> x0, blocking collectives: 46 us -> none  [the longest x1 29 us: body(): lax.all_to_all(gate_grad, 'tp', split_axis=0, concat_axis=1, tiled=True)]
    broadcast_in_dim x10 -> x1, local copies, waits for them, and re-layouts: 14 us -> 0.01 us  [body(): zero = jnp.zeros((width, 64), BF16)]
    dot_general x10 -> x6, matrix products: 18.8 us -> 8.13 us  [dot(): lax.dot_general(a, b, (((ca,), (cb,)), ((), ())), preferred_element_type=...]
    unnamed x36 -> x24, local copies, waits for them, and re-layouts: 3.73 us -> 12.8 us
    reduce_sum x8 -> x0, other arithmetic: 6.72 us -> none  [the longest x2 4.23 us: sum_at_owner(): return jnp.sum(pieces.astype(jnp.float32), axis=0)]
  transfers between devices with their start and end apart: 9 -> 0, of which waited for: 8 -> 0; matrix products, arithmetic and copies ran while one was open for 13% -> 0% of each run, Pallas kernels for 0% -> 0%
where the time goes in v1:
time: 159 us; the launch traced here: 158 us
  Pallas kernels  122 us (77%)
  local copies, waits for them, and re-layouts  21.9 us (14%)
  matrix products  8.13 us (5%)
  other arithmetic  5.59 us (4%)
    pallas_call x1, Pallas kernels, back(): pl.pallas_call(back_kernel, out_shape=(jax.ShapeDtypeStruct((width, n * s...  82.9 us
    pallas_call x1, Pallas kernels, dispatch(): pl.pallas_call(dispatch_kernel, out_shape=(jax.ShapeDtypeStruct((width, P...  39.1 us
    unnamed x24, local copies, waits for them, and re-layouts  12.8 us
    dot_general x6, matrix products, dot(): lax.dot_general(a, b, (((ca,), (cb,)), ((), ())), preferred_element_type=...  8.13 us
    concatenate x1, local copies, waits for them, and re-layouts, body(): part = jnp.concatenate([out, grad[:, 256:], grad[:, :256]], axis=1)  6.17 us

profile of v1, /device:TPU:1, one launch (start us, length us, event | category | flops | bytes accessed | tf_op | source)
XLA Modules:
  0.0 158.4 jit_solution(8121513480204975891)
XLA Ops:
  0.6 0.0 copy-start
  0.7 0.1 fusion.37
  0.7 1.5 copy.13.ids_ref
  2.2 1.4 copy.14.w_ref
  3.6 39.1 %dispatch.1 = (bf16[96,640]{1,0:T(8,128)(2,1)}, bf16[3072,640]{1,0:T(8,128)(2,1)}) custom-call(bf16[96,96]{1,0:T(8,128)(2,1)} %tok_ref.1, bf16[96,96]{1,0:T(8,128)(2,1)} %cot_ref.3, s32[96,2]{1,0:T(8,128)} %copy.13.ids_ref, f32[96,2]{1,0:T(8,128)} %copy.14.w_ref), custom_call_target="tpu_custom_call" | custom-call | tf_op jit(solution)/shard_map/dispatch/pallas_call | solution.py:299
  42.7 0.7 slice.66
  43.4 0.8 slice.67
  44.2 1.6 %pad_maximum_fusion.3 = (bf16[96,384]{1,0:T(8,128)(2,1)}, bf16[96,384]{1,0:T(8,128)(2,1)}) fusion(bf16[96,256]{1,0:T(8,128)(2,1)S(1)} %slice.67, bf16[96,64]{1,0:T(8,128)(2,1)S(1)} %slice.66, bf16[384]{0:T(512)(128)(2,1)S(1)} %get-tuple-element.34, bf16[96,640]{1,0:T(8,128)(2,1)} %get-tuple-element.15, pred[384]{0:T(512)(128)(4,1)} %constant.9.clone.1), kind=kLoop, calls=%fused_computation.34 | loop fusion | flops 258048 | bytes 283776 | tf_op jit(solution)/shard_map/concatenate | solution.py:505
  45.9 1.1 copy.20
  46.9 0.8 maximum_bitcast_fusion.dy_ref
  47.7 0.0 copy-start.1
  47.7 0.0 copy-start.7
  47.7 3.3 %fusion.21 = f32[256,384]{1,0:T(8,128)S(1)} fusion(bf16[1,3072,256]{2,1,0:T(8,128)(2,1)} %param.12, bf16[3072,640]{1,0:T(8,128)(2,1)} %get-tuple-element.14), kind=kOutput, calls=%fused_computation.20 | convolution fusion | flops 603979776 | bytes 4325376 | tf_op jit(solution)/shard_map/dot_general | solution.py:25
  51.0 0.0 copy-done.1
  51.0 0.5 copy-done.7
  51.5 1.0 fusion.26
  52.5 0.1 fusion.36
  52.6 0.0 copy-done
  52.6 1.2 select_convert_fusion
  53.9 0.9 pad_maximum_fusion.1.act_ref
  54.8 0.7 fusion.1
  55.5 0.0 copy-start.4
  55.5 1.0 fusion.13
  56.5 0.4 copy-done.4
  56.9 1.0 fusion.2
  57.9 0.1 slice.80
  58.1 2.3 %pad_maximum_fusion = bf16[3072,640]{0,1:T(8,128)(2,1)} fusion(bf16[3072,256]{0,1:T(8,128)(2,1)S(1)} %slice.80, bf16[3072,64]{0,1:T(8,128)(2,1)S(1)} %slice.79, bf16[3072,320]{0,1:T(8,128)(2,1)S(1)} %fusion.1), kind=kLoop, calls=%fused_computation.3 | loop fusion | flops 11796480 | bytes 7864320 | tf_op jit(solution)/shard_map/concatenate | solution.py:502
  60.3 6.2 %copy.18 = bf16[3072,640]{1,0:T(8,128)(2,1)} copy(bf16[3072,640]{0,1:T(8,128)(2,1)} %pad_maximum_fusion) | data formatting | bytes 7864320 | tf_op jit(solution)/shard_map/concatenate | solution.py:502
  66.5 82.9 %back.1 = (bf16[96,8192]{1,0:T(8,128)(2,1)}, bf16[96,8192]{1,0:T(8,128)(2,1)}, bf16[8192,96]{1,0:T(8,128)(2,1)}, bf16[96,96]{1,0:T(8,128)(2,1)}, bf16[96,96]{1,0:T(8,128)(2,1)}, /*index=5*/f32[96,2]{1,0:T(8,128)}) custom-call(bf16[16,2,96,640]{3,2,1,0:T(8,128)(2,1)} %bitcast.41, bf16[256,1024]{1,0:T(8,128)(2,1)} %pad_maximum_fusion.1.act_ref, ...), custom_call_target="tpu_custom_call" | custom-call | tf_op jit(solution)/shard_map/back/pallas_call | solution.py:451
  149.4 0.0 copy-start.6
  149.4 0.0 copy-start.5
  149.4 0.0 copy-start.3
  149.4 1.6 copy.24
  150.9 3.9 %copy.25 = bf16[1,8192,96]{1,2,0:T(8,128)(2,1)} copy(bf16[1,8192,96]{2,1,0:T(8,128)(2,1)} %bitcast.42) | data formatting | bytes 3145728
  154.8 0.0 copy-done.6
  154.9 0.0 copy-start.2
  154.9 0.6 copy.33
  155.5 0.0 copy-done.5
  155.5 0.6 copy.34
  156.1 0.0 copy-done.3
  156.1 1.1 copy.35
  157.2 0.0 copy-done.2
  157.2 1.1 copy.36
  (9 shorter events, 0.1 us)
Async XLA Ops:
  0.6 52.0 %copy-start = (bf16[1,3072,256]{2,1,0:T(8,128)(2,1)S(1)}, bf16[1,3072,256]{2,1,0:T(8,128)(2,1)}, u32[]{:S(2)}) copy-start(bf16[1,3072,256]{2,1,0:T(8,128)(2,1)} %param.11) | copy-start | bytes 4718596
  47.7 3.3 %copy-start.1 = (bf16[1,256,3072]{2,1,0:T(8,128)(2,1)S(1)}, bf16[1,256,3072]{2,1,0:T(8,128)(2,1)}, u32[]{:S(2)}) copy-start(bf16[1,256,3072]{2,1,0:T(8,128)(2,1)} %param.13) | copy-start | bytes 4718596
  47.7 3.8 %copy-start.7 = (bf16[3072,640]{1,0:T(8,128)(2,1)S(1)}, bf16[3072,640]{1,0:T(8,128)(2,1)}, u32[]{:S(2)}) copy-start(bf16[3072,640]{1,0:T(8,128)(2,1)} %get-tuple-element.14) | copy-start | bytes 11796484
  55.5 1.4 copy-start.4
  149.4 5.5 %copy-start.6 = (bf16[96,96]{1,0:T(8,128)(2,1)S(1)}, bf16[96,96]{1,0:T(8,128)(2,1)}, u32[]{:S(2)}) copy-start(bf16[96,96]{1,0:T(8,128)(2,1)} %get-tuple-element.43) | copy-start | bytes 55300
  149.4 6.1 %copy-start.5 = (bf16[96,96]{1,0:T(8,128)(2,1)S(1)}, bf16[96,96]{1,0:T(8,128)(2,1)}, u32[]{:S(2)}) copy-start(bf16[96,96]{1,0:T(8,128)(2,1)} %get-tuple-element.44) | copy-start | bytes 55300
  149.4 6.7 %copy-start.3 = (bf16[96,8192]{1,0:T(8,128)(2,1)S(1)}, bf16[96,8192]{1,0:T(8,128)(2,1)}, u32[]{:S(2)}) copy-start(bf16[96,8192]{1,0:T(8,128)(2,1)} %get-tuple-element.19) | copy-start | bytes 4718596
  154.9 2.4 %copy-start.2 = (bf16[96,8192]{1,0:T(8,128)(2,1)S(1)}, bf16[96,8192]{1,0:T(8,128)(2,1)}, u32[]{:S(2)}) copy-start(bf16[96,8192]{1,0:T(8,128)(2,1)} %get-tuple-element.20) | copy-start | bytes 4718596

commit v2 on v1

--- a/solution.py
+++ b/solution.py
@@ -9,7 +9,7 @@
 
 SIDE = 4
 CAP = 40
-HALF = 48
+HALF = CAP
 PAIR = 2 * HALF
 GROUPS = 8
 ROWS = GROUPS * PAIR
@@ -85,28 +85,31 @@
     barrier = pltpu.get_barrier_semaphore()
     for to in partners:
         pl.semaphore_signal(barrier, inc=1, device_id=to, device_id_type=pl.DeviceIdType.MESH)
-    pl.semaphore_wait(barrier, len(partners))
-
-
-def gather(g, cp, half, part, tick):
+
+
+def greeted(partners):
+    pl.semaphore_wait(pltpu.get_barrier_semaphore(), len(partners))
+
+
+def gather(g, cp, name, half, part, tick):
     sib = {"tp": g.at(0, 0, True)}
 
     def nbr(h, axis, d):
         return {"tp": g.block(h, d, 0) if axis == 1 else g.block(h, 0, d)}
 
     def send(key, h, axis, d, ref):
-        cp.start(key, ref, ref, nbr(h, axis, d))
+        cp.start((name, *key), ref, ref, nbr(h, axis, d))
 
     def got(key, h, axis, d, ref):
-        cp.wait(key, ref, nbr(h, axis, d))
+        cp.wait((name, *key), ref, nbr(h, axis, d))
 
     def across(h, o1, o2):
         ref = half(g.block(h, o1, o2), h)
-        cp.start(("s", h, o1, o2), ref, ref, sib)
+        cp.start((name, "s", h, o1, o2), ref, ref, sib)
 
     def from_sib(h, o1, o2):
         b = g.block(h, o1, o2, True)
-        cp.wait(("s", h, o1, o2), half(b, h), sib)
+        cp.wait((name, "s", h, o1, o2), half(b, h), sib)
         tick(b, h)
 
     dirs = (1, -1)
@@ -205,30 +208,41 @@
     yield
 
 
+def column(row):
+    n = row.shape[1]
+    eye = iota((n, n), 0) == iota((n, n), 1)
+    return jnp.sum(jnp.where(eye, row, jnp.zeros_like(row)), axis=1, keepdims=True)
+
+
+def as_row(col):
+    n = col.shape[0]
+    eye = iota((n, n), 0) == iota((n, n), 1)
+    return jnp.sum(jnp.where(eye, col, jnp.zeros_like(col)), axis=0, keepdims=True)
+
+
 def places(ids):
-    n = ids.shape[0]
-    lane = iota((n, 128), 1)
+    n = ids[0].shape[0]
+    lane = iota((n, 128), 1).astype(F32)
     before = (iota((n, n), 1) < iota((n, n), 0)).astype(BF16)
-    hot = [(ids[:, k : k + 1] == lane).astype(F32) for k in (0, 1)]
+    hot = [(ids[k] == lane).astype(F32) for k in (0, 1)]
     seen = [dot(before, hot[k].astype(BF16), 1, 0) for k in (0, 1)]
     seen[1] = seen[1] + jnp.sum(hot[0], axis=0, keepdims=True)
     rank = [jnp.sum(seen[k] * hot[k], axis=1, keepdims=True) for k in (0, 1)]
-    row = [ids[:, k : k + 1].astype(F32) * PAIR + rank[k] for k in (0, 1)]
+    row = [ids[k] * PAIR + rank[k] for k in (0, 1)]
     lanes = iota((n, ROWS), 1).astype(F32)
     first = [(lanes == row[k]).astype(BF16) for k in (0, 1)]
     second = [(lanes == row[k] + HALF).astype(BF16) for k in (0, 1)]
     return first, second
 
 
-def packing():
-    r = iota((ROWS, PACK), 0)
-    lane = iota((ROWS, PACK), 1)
-    j = r % PAIR
-    grad = j >= HALF
-    k = jnp.where(grad, j - HALF, j)
-    s = (r // PAIR) * CAP + k
-    want = jnp.where(grad, jnp.where(s < 256, s + 384, s + 64), s)
-    return ((want == lane) & (k < CAP)).astype(BF16)
+def fill_packing(pack):
+    j = iota((PAIR, 1), 0)
+    lane = iota((PAIR, PACK), 1)
+    for z in range(GROUPS):
+        s = z * CAP + j
+        d = s - CAP
+        want = jnp.where(j >= CAP, jnp.where(d < 256, d + 384, d + 64), s)
+        pack[z * PAIR : (z + 1) * PAIR, :] = (want == lane).astype(F32).astype(BF16)
 
 
 def to_all_groups(g, cp, src, dst, name):
@@ -253,88 +267,116 @@
     dst[mine] = src[mine]
 
 
-def dispatch_kernel(tok_ref, cot_ref, ids_ref, w_ref, own_ref, all_ref, rows, got, send, recv):
+def turned(t):
+    return pltpu.roll(t, 64, 1)
+
+
+def layer_kernel(
+    tok_ref, cot_ref, ids_ref, w_ref, gw_hbm, uw_hbm, dw_hbm,
+    gate_ref, up_ref, down_ref, mixed_ref, gt_ref, gc_ref,
+    gw, uw, dw, gwt, uwt, dwt, pack, all_ref, win, hx, gy, uy,
+    full, part_ref, sib, chip, ra, rb, mid, fin, rows, got, rows2, got2, red, local, send, recv,
+):
     g = Grid()
     cp = Copies(send, recv)
-    greet(
-        [{"tp": g.at(0, 0, True)}]
-        + [{"tp": g.at(*o)} for o in ((0, 1), (0, -1), (1, 0), (-1, 0))]
-        + [{"ep": g.up(k)} for k in range(1, GROUPS)]
+    sib_dev = {"tp": g.at(0, 0, True)}
+    ring = ((0, 1), (0, -1), (0, 2), (1, 0), (-1, 0), (2, 0))
+    partners = (
+        [sib_dev] + [{"tp": g.at(*o)} for o in ring] + [{"ep": g.up(k)} for k in range(1, GROUPS)]
     )
-    first, second = places(ids_ref[...])
+    greet(partners)
+    loads = [
+        pltpu.make_async_copy(a, b, local.at[i])
+        for i, (a, b) in enumerate(((gw_hbm, gw), (uw_hbm, uw), (dw_hbm, dw)))
+    ]
+    for c in loads:
+        c.start()
+
+    width = tok_ref.shape[1]
+    ids = [column(ids_ref[k : k + 1, :].astype(F32)) for k in (0, 1)]
+    w = [column(w_ref[k : k + 1, :]) for k in (0, 1)]
+    first, second = places(ids)
     cot = cot_ref[...].astype(F32)
-    w = w_ref[...]
-    scaled = [(w[:, k : k + 1] * cot).astype(BF16) for k in (0, 1)]
+    scaled = [(w[k] * cot).astype(BF16) for k in (0, 1)]
     sent = dot(first[0] + first[1], tok_ref[...], 0, 0)
     sent = sent + dot(second[0], scaled[0], 0, 0) + dot(second[1], scaled[1], 0, 0)
     rows[...] = sent.astype(BF16)
+    greeted(partners)
     to_all_groups(g, cp, rows, got, "out")
     own_group(g, rows, got)
-    pack = packing()
+    fill_packing(pack)
+    for c in loads:
+        c.wait()
+    size = gw.shape[1]
+    blocks = gw.shape[0] // width
+
+    def turn(i, _):
+        at = pl.ds(pl.multiple_of(i * 256, 256), 256)
+        gwt[:, at] = gw[at, :].T
+        uwt[:, at] = uw[at, :].T
+        dwt[at, :] = dw[:, at].T
+        return _
+
+    lax.fori_loop(0, gw.shape[0] // 256, turn, 0)
     from_all_groups(g, cp, got, "out")
-    own = dot(got[...], pack, 0, 0).astype(BF16)
-    own_ref[...] = own
-    size = own.shape[0]
-    all_ref[pl.ds(pl.multiple_of(g.tp * size, size), size), :] = own
+    own = dot(got[...], pack[...], 0, 0)
+    all_ref[pl.ds(pl.multiple_of(g.tp * width, width), width), :] = own.astype(BF16)
+    low = iota((width, 128), 1) < 64
+    o = [own[:, i * 128 : (i + 1) * 128] for i in range(5)]
+    x2 = jnp.where(low, o[2], 0.0)
+    d2 = jnp.where(low, turned(o[2]), 0.0)
+    for i, t in enumerate((turned(x2), o[0], o[1])):
+        win[0, :, i * 128 : (i + 1) * 128] = t.astype(BF16)
+    for i, t in enumerate((o[0], o[1], x2)):
+        win[1, :, i * 128 : (i + 1) * 128] = t.astype(BF16)
+    for i, t in enumerate((o[3], o[4], d2)):
+        win[2, :, i * 128 : (i + 1) * 128] = t.astype(BF16)
+    half_w = width // 2
+
+    def half_in(b, h):
+        return all_ref.at[pl.ds(pl.multiple_of(b * width + h * half_w, 16), half_w)]
+
+    def part_in(b, h, q, o):
+        rng = pl.ds(0, 384) if (q > 0) == (o in (0, 1)) else pl.ds(384, 256)
+        return all_ref.at[pl.ds(pl.multiple_of(b * width + h * half_w, 16), half_w), rng]
+
+    for _ in gather(g, cp, "in", half_in, part_in, lambda b, h: None):
+        pass
+
     hh = size // 2
-
-    def half(b, h):
-        return all_ref.at[pl.ds(pl.multiple_of(b * size + h * hh, 16), hh)]
-
-    def part(b, h, q, o):
-        low = (q > 0) == (o in (0, 1))
-        rng = pl.ds(0, 384) if low else pl.ds(384, 256)
-        return all_ref.at[pl.ds(pl.multiple_of(b * size + h * hh, 16), hh), rng]
-
-    for _ in gather(g, cp, half, part, lambda b, h: None):
-        pass
-    cp.finish()
-
-
-N_DISPATCH = 7 + 40 + 32
-
-
-def dispatch(tokens, cotangent, ids, weights):
-    width = tokens.shape[1]
-    return pl.pallas_call(
-        dispatch_kernel,
-        out_shape=(
-            jax.ShapeDtypeStruct((width, PACK), BF16),
-            jax.ShapeDtypeStruct((2 * SIDE * SIDE * width, PACK), BF16),
-        ),
-        in_specs=[VMEM] * 4,
-        out_specs=(VMEM, VMEM),
-        scratch_shapes=[
-            pltpu.VMEM((ROWS, width), BF16),
-            pltpu.VMEM((ROWS, width), BF16),
-            pltpu.SemaphoreType.DMA((N_DISPATCH,)),
-            pltpu.SemaphoreType.DMA((N_DISPATCH,)),
-        ],
-        compiler_params=pltpu.CompilerParams(
-            collective_id=0, has_side_effects=True, vmem_limit_bytes=60 * 2**20
-        ),
-        name="dispatch",
-    )(tokens, cotangent, ids, weights)
-
-
-def back_kernel(
-    part_ref, act_ref, xg_ref, xu_ref, dy_ref, cot_ref, ids_ref, w_ref,
-    gate_ref, up_ref, down_ref, mixed_ref, gt_ref, gc_ref,
-    full, sib, chip, ra, rb, mid, fin, rows, got, red, send, recv,
-):
-    g = Grid()
-    cp = Copies(send, recv)
-    ring = ((0, 1), (0, -1), (0, 2), (1, 0), (-1, 0), (2, 0))
-    greet(
-        [{"tp": g.at(0, 0, True)}]
-        + [{"tp": g.at(*o)} for o in ring]
-        + [{"ep": g.up(k)} for k in range(1, GROUPS)]
-    )
-    size = act_ref.shape[0]
-    hh = size // 2
-    width = part_ref.shape[2]
-    half_w = width // 2
-    sib_dev = {"tp": g.at(0, 0, True)}
+    mine = g.tp * size
+
+    def units(h, _):
+        r = pl.ds(pl.multiple_of(h * hh, hh), hh)
+        gate = dot(gwt[r, :], all_ref[:, :WIN], 1, 0)
+        upp = dot(uwt[r, :], all_ref[:, :WIN], 1, 0)
+        gh = dot(dw[r, :], all_ref[:, 256:], 1, 0)
+        at = pl.ds(pl.multiple_of(mine + h * hh, hh), hh)
+        lo = iota((hh, 128), 1) < 64
+        for i in range(3):
+            t = slice(i * 128, (i + 1) * 128)
+            gp, u = gate[:, t], upp[:, t]
+            d = turned(gh[:, 0:128]) if i == 2 else gh[:, (i + 1) * 128 : (i + 2) * 128]
+            s = jax.nn.sigmoid(gp)
+            active = gp * s
+            hid = active * u
+            gg = d * u * (s * (1.0 + gp * (1.0 - s)))
+            gu = d * active
+            if i == 2:
+                hid, gg, gu = (jnp.where(lo, a, 0.0) for a in (hid, gg, gu))
+                full[at, 256:384] = (hid + turned(gg)).astype(BF16)
+                gy[r, 0:128] = turned(gg).astype(BF16)
+                uy[r, 0:128] = turned(gu).astype(BF16)
+            else:
+                full[at, t] = hid.astype(BF16)
+                full[at, 384 + i * 128 : 512 + i * 128] = gg.astype(BF16)
+                gy[r, (i + 1) * 128 : (i + 2) * 128] = gg.astype(BF16)
+                uy[r, (i + 1) * 128 : (i + 2) * 128] = gu.astype(BF16)
+            hx[r, t] = hid.astype(BF16)
+            full[at, 640 + i * 128 : 768 + i * 128] = gu.astype(BF16)
+        return _
+
+    lax.fori_loop(0, 2, units, 0)
 
     def half(b, h):
         return full.at[pl.ds(pl.multiple_of(b * size + h * hh, 64), hh)]
@@ -346,17 +388,32 @@
     def tick(b, h):
         at = pl.multiple_of(b * size + h * hh, 128)
         blk = full[pl.ds(at, hh), :]
-        down_ref[pl.ds(at, hh), :] = dot(blk[:, :WIN], dy_ref[...], 1, 0).astype(BF16)
-        gate_ref[:, pl.ds(at, hh)] = dot(xg_ref[...], blk[:, 256:640], 1, 1).astype(BF16)
-        up_ref[:, pl.ds(at, hh)] = dot(xu_ref[...], blk[:, 640:], 1, 1).astype(BF16)
-
-    cp.start("pair", part_ref.at[:, 1 - g.c], sib, sib_dev)
-    mine = pl.ds(pl.multiple_of(g.tp * size, 256), size)
-    full[mine, :] = act_ref[...]
+        gate_ref[:, pl.ds(at, hh)] = dot(win[0], blk[:, 256:640], 1, 1).astype(BF16)
+        up_ref[:, pl.ds(at, hh)] = dot(win[1], blk[:, 640:], 1, 1).astype(BF16)
+        down_ref[:, pl.ds(at, hh)] = dot(win[2], blk[:, :WIN], 1, 1).astype(BF16)
+
+    steps = gather(g, cp, "act", half, part, tick)
+    next(steps)
+
+    def partial(c):
+        def one(i, _):
+            at = pl.ds(pl.multiple_of((2 * i + c) * width, width), width)
+            out = dot(dwt[at, :], hx[...], 1, 0)
+            inn = dot(gw[at, :], gy[...], 1, 0) + dot(uw[at, :], uy[...], 1, 0)
+            part_ref[c, i, :, 0:256] = out[:, 0:256].astype(BF16)
+            part_ref[c, i, :, 256:384] = (out[:, 256:] + inn[:, :128]).astype(BF16)
+            part_ref[c, i, :, 384:640] = inn[:, 128:].astype(BF16)
+            return _
+
+        lax.fori_loop(0, blocks // 2, one, 0)
+
+    partial(1 - g.c)
+    cp.start("pair", part_ref.at[1 - g.c], sib, sib_dev)
+    partial(g.c)
     cp.wait("pair", sib, sib_dev)
 
     def add_pair(i, _):
-        chip[i] = (part_ref[i, g.c].astype(F32) + sib[i].astype(F32)).astype(BF16)
+        chip[i] = (part_ref[g.c, i].astype(F32) + sib[i].astype(F32)).astype(BF16)
         return _
 
     lax.fori_loop(0, SIDE * SIDE, add_pair, 0)
@@ -372,7 +429,6 @@
         cp.start(("a1", d), chip.at[pl.ds(y_of(d) * SIDE, SIDE), lo], ra.at[i], {"tp": g.at(d, 0)})
         for r in range(SIDE):
             cp.start(("b1", d, r), chip.at[r * SIDE + x_of(d), hi], rb.at[i, r], {"tp": g.at(0, d)})
-    steps = gather(g, cp, half, part, tick)
     next(steps)
     for i, d in enumerate((1, -1, 2)):
         cp.wait(("a1", d), ra.at[i], {"tp": g.at(-d, 0)})
@@ -405,22 +461,20 @@
         for i in range(3):
             s = s + fin[h, i].astype(F32)
         sums.append(s)
-    own = jnp.concatenate(sums, axis=0).astype(BF16)
-    rows[...] = dot(packing(), own, 1, 1).astype(BF16)
-    to_all_groups(g, cp, rows, got, "back")
-    own_group(g, rows, got)
-    next(steps)
-    first, second = places(ids_ref[...])
-    from_all_groups(g, cp, got, "back")
-    back = got[...]
-    cot = cot_ref[...].astype(F32)
-    w = w_ref[...]
+    total = jnp.concatenate(sums, axis=0).astype(BF16)
+    rows2[...] = dot(pack[...], total, 1, 1).astype(BF16)
+    to_all_groups(g, cp, rows2, got2, "back")
+    own_group(g, rows2, got2)
+    next(steps)
+    from_all_groups(g, cp, got2, "back")
+    back = got2[...]
     outs = [dot(first[k], back, 1, 0) for k in (0, 1)]
-    mixed_ref[...] = (w[:, 0:1] * outs[0] + w[:, 1:2] * outs[1]).astype(BF16)
+    mixed_ref[...] = (w[0] * outs[0] + w[1] * outs[1]).astype(BF16)
     gt_ref[...] = (dot(second[0], back, 1, 0) + dot(second[1], back, 1, 0)).astype(BF16)
-    inner = [jnp.sum(cot * outs[k], axis=1, keepdims=True) for k in (0, 1)]
-    lane = iota((inner[0].shape[0], 128), 1)
-    red[0] = jnp.where(lane == 0, inner[0], jnp.where(lane == 1, inner[1], 0.0))
+    inner = [as_row(jnp.sum(cot * outs[k], axis=1, keepdims=True)) for k in (0, 1)]
+    sub = iota((8, width), 0)
+    red[0] = jnp.zeros((8, 128), F32)
+    red[0, :, 0:width] = jnp.where(sub == 0, inner[0], jnp.where(sub == 1, inner[1], 0.0))
     cp.start("g0", red.at[0], red.at[1], sib_dev)
     next(steps)
     cp.wait("g0", red.at[1], sib_dev)
@@ -437,31 +491,46 @@
         pass
     for d in (1, -1, 2):
         cp.wait(("g2", d), red.at[6 + y_of(-d)], {"tp": g.at(-d, 0)})
-    gc_ref[...] = ((red[6] + red[7]) + (red[8] + red[9]))[:, :2]
+    gc_ref[...] = ((red[6] + red[7]) + (red[8] + red[9]))[0:2, 0:width]
     cp.finish()
 
 
-N_BACK = 1 + 15 + 72 + 6 + 7 + 7
-
-
-def back(part, act, xg, xu, dy, cotangent, ids, weights):
-    width = cotangent.shape[1]
-    size = act.shape[0]
-    n = 2 * SIDE * SIDE
+N_COPIES = 2 * 7 + 2 * (40 + 32) + 1 + 15 + 6 + 7
+
+
+def layer(tokens, cotangent, ids, weights, gate_w, up_w, down_w):
+    width = tokens.shape[1]
+    model, size = gate_w.shape
+    n = model // width
+    wide = jax.ShapeDtypeStruct((width, n * size), BF16)
+    ANY = pl.BlockSpec(memory_space=pl.ANY)
     return pl.pallas_call(
-        back_kernel,
+        layer_kernel,
         out_shape=(
-            jax.ShapeDtypeStruct((width, n * size), BF16),
-            jax.ShapeDtypeStruct((width, n * size), BF16),
-            jax.ShapeDtypeStruct((n * size, width), BF16),
+            wide,
+            wide,
+            wide,
             jax.ShapeDtypeStruct(cotangent.shape, BF16),
             jax.ShapeDtypeStruct(cotangent.shape, BF16),
             jax.ShapeDtypeStruct(ids.shape, F32),
         ),
-        in_specs=[VMEM] * 8,
+        in_specs=[VMEM] * 4 + [ANY] * 3,
         out_specs=(VMEM,) * 6,
         scratch_shapes=[
-            pltpu.VMEM((n * size, act.shape[1]), BF16),
+            pltpu.VMEM((model, size), BF16),
+            pltpu.VMEM((model, size), BF16),
+            pltpu.VMEM((size, model), BF16),
+            pltpu.VMEM((size, model), BF16),
+            pltpu.VMEM((size, model), BF16),
+            pltpu.VMEM((model, size), BF16),
+            pltpu.VMEM((ROWS, PACK), BF16),
+            pltpu.VMEM((model, PACK), BF16),
+            pltpu.VMEM((3, width, WIN), BF16),
+            pltpu.VMEM((size, WIN), BF16),
+            pltpu.VMEM((size, WIN), BF16),
+            pltpu.VMEM((size, WIN), BF16),
+            pltpu.VMEM((n * size, 1024), BF16),
+            pltpu.VMEM((2, SIDE * SIDE, width, PACK), BF16),
             pltpu.VMEM((SIDE * SIDE, width, PACK), BF16),
             pltpu.VMEM((SIDE * SIDE, width, PACK), BF16),
             pltpu.VMEM((3, SIDE, width // 2, PACK), BF16),
@@ -470,45 +539,25 @@
             pltpu.VMEM((2, 3, width // 2, PACK), BF16),
             pltpu.VMEM((ROWS, width), BF16),
             pltpu.VMEM((ROWS, width), BF16),
-            pltpu.VMEM((10, width, 128), F32),
-            pltpu.SemaphoreType.DMA((N_BACK,)),
-            pltpu.SemaphoreType.DMA((N_BACK,)),
+            pltpu.VMEM((ROWS, width), BF16),
+            pltpu.VMEM((ROWS, width), BF16),
+            pltpu.VMEM((10, 8, 128), F32),
+            pltpu.SemaphoreType.DMA((3,)),
+            pltpu.SemaphoreType.DMA((N_COPIES,)),
+            pltpu.SemaphoreType.DMA((N_COPIES,)),
         ],
         compiler_params=pltpu.CompilerParams(
-            collective_id=1, has_side_effects=True, vmem_limit_bytes=60 * 2**20
+            collective_id=0, has_side_effects=True, vmem_limit_bytes=63 * 2**20
         ),
-        name="back",
-    )(part, act, xg, xu, dy, cotangent, ids, weights)
+        name="layer",
+    )(tokens, cotangent, ids, weights, gate_w, up_w, down_w)
 
 
 def body(tokens, cotangent, expert_ids, combine_weights, w_gate, w_up, w_down):
-    width = tokens.shape[1]
-    gate_w, up_w, down_w = w_gate[0], w_up[0], w_down[0]
-    own, xd = dispatch(tokens, cotangent, expert_ids, combine_weights)
-    gate_pre = dot(gate_w, xd[:, :WIN], 0, 0)
-    up_pre = dot(up_w, xd[:, :WIN], 0, 0)
-    gh = dot(down_w, xd[:, 256:], 1, 0)
-    gh = jnp.concatenate([gh[:, 128:], gh[:, 64:128], gh[:, 0:64]], axis=1)
-    live = iota(gh.shape, 1) < SLOTS
-    sigma = jax.nn.sigmoid(gate_pre)
-    active = gate_pre * sigma
-    slope = sigma * (1.0 + gate_pre * (1.0 - sigma))
-    hidden = jnp.where(live, active * up_pre, 0.0).astype(BF16)
-    ggp = jnp.where(live, gh * up_pre * slope, 0.0).astype(BF16)
-    gup = jnp.where(live, gh * active, 0.0).astype(BF16)
-    act = jnp.concatenate([hidden[:, :SLOTS], ggp[:, 256:SLOTS], ggp[:, :256], gup], axis=1)
-    out = dot(down_w, hidden[:, :SLOTS], 0, 0).astype(BF16)
-    grad = (dot(gate_w, ggp[:, :SLOTS], 1, 0) + dot(up_w, gup[:, :SLOTS], 1, 0)).astype(BF16)
-    part = jnp.concatenate([out, grad[:, 256:], grad[:, :256]], axis=1)
-    part = part.reshape(SIDE * SIDE, 2, width, PACK)
-    zero = jnp.zeros((width, 64), BF16)
-    xg = jnp.concatenate([zero, own[:, 256:320], own[:, :256]], axis=1)
-    xu = jnp.concatenate([own[:, :320], zero], axis=1)
-    dy = jnp.concatenate([own[:, 384:], own[:, 320:384], zero], axis=1).T
-    gate, up, down, mixed, gt, gc = back(
-        part, act, xg, xu, dy, cotangent, expert_ids, combine_weights
+    gate, up, down, mixed, gt, gc = layer(
+        tokens, cotangent, expert_ids.T, combine_weights.T, w_gate[0], w_up[0], w_down[0]
     )
-    return mixed, gt, gc, gate[None], up[None], down[None]
+    return mixed, gt, gc.T, gate[None], up[None], down.T[None]
 
 
 def solution(mesh):

time: 159 us -> 116 us (0.73)
  Pallas kernels: 122 us -> 105 us
  local copies, waits for them, and re-layouts: 21.9 us -> 9.81 us
  matrix products: 8.13 us -> 0 us
  other arithmetic: 5.59 us -> 0 us
    pallas_call x2 -> x1, Pallas kernels: 122 us -> 105 us  [layer(): pl.pallas_call(layer_kernel, out_shape=(wide, wide, wide, jax.ShapeDtypeS...]
    dot_general x6 -> x0, matrix products: 8.13 us -> none  [dot(): lax.dot_general(a, b, (((ca,), (cb,)), ((), ())), preferred_element_type=...]
    concatenate x2 -> x0, local copies, waits for them, and re-layouts: 6.25 us -> none  [the longest x1 6.17 us: body(): part = jnp.concatenate([out, grad[:, 256:], grad[:, :256]], axis=1)]
    concatenate x3 -> x0, other arithmetic: 4.78 us -> none  [the longest x1 2.25 us: body(): part = jnp.concatenate([out, grad[:, 256:], grad[:, :256]], axis=1)]
    unnamed x24 -> x10, local copies, waits for them, and re-layouts: 12.8 us -> 9.81 us
    slice x10 -> x0, local copies, waits for them, and re-layouts: 1.81 us -> none  [the longest x2 1.54 us: body(): xg = jnp.concatenate([zero, own[:, 256:320], own[:, :256]], axis=1)]
where the time goes in v2:
time: 116 us
  Pallas kernels  105 us (91%)
  local copies, waits for them, and re-layouts  9.81 us (8%)
    pallas_call x1, Pallas kernels, layer(): pl.pallas_call(layer_kernel, out_shape=(wide, wide, wide, jax.ShapeDtypeS...  105 us
    unnamed x10, local copies, waits for them, and re-layouts  9.81 us

profile of v2, /device:TPU:1, one launch (start us, length us, event | category | flops | bytes accessed | tf_op | source)
XLA Modules:
  0.0 115.6 jit_solution(4869695946003530933)
XLA Ops:
  0.6 105.1 %layer.1 = (bf16[96,8192]{1,0:T(8,128)(2,1)}, bf16[96,8192]{1,0:T(8,128)(2,1)}, bf16[96,8192]{1,0:T(8,128)(2,1)}, bf16[96,96]{1,0:T(8,128)(2,1)}, bf16[96,96]{1,0:T(8,128)(2,1)}, /*index=5*/f32[2,96]{1,0:T(2,128)}) custom-call(bf16[96,96]{1,0:T(8,128)(2,1)} %tok_ref.1, bf16[96,96]{1,0:T(8,128)(2,1)} %cot_ref.1, s32[2,96]{1,0:T(2,128)} %bitcast.17, ...), custom_call_target="tpu_custom_call" | custom-call | tf_op jit(solution)/shard_map/layer/pallas_call | solution.py:507
  105.8 1.3 %copy.19 = bf16[96,96]{1,0:T(8,128)(2,1)} copy(bf16[96,96]{1,0:T(8,128)(2,1)} %get-tuple-element.24) | data formatting | bytes 36864
  107.1 1.3 %copy.20 = bf16[96,96]{1,0:T(8,128)(2,1)} copy(bf16[96,96]{1,0:T(8,128)(2,1)} %get-tuple-element.25) | data formatting | bytes 36864
  108.5 1.2 %copy.21 = f32[96,2]{0,1:T(2,128)} copy(f32[96,2]{0,1:T(2,128)} %bitcast.19) | data formatting | bytes 1536
  109.7 0.0 copy-start.1
  109.7 2.8 %copy.22 = bf16[1,96,8192]{2,1,0:T(8,128)(2,1)} copy(bf16[1,96,8192]{2,1,0:T(8,128)(2,1)} %bitcast.13) | data formatting | bytes 3145728
  112.5 0.0 copy-done.1
  112.5 0.0 copy-start
  112.5 1.1 copy.23
  113.6 0.8 copy-done
  114.5 1.1 copy.24
Async XLA Ops:
  109.7 2.8 %copy-start.1 = (bf16[96,8192]{1,0:T(8,128)(2,1)S(1)}, bf16[96,8192]{1,0:T(8,128)(2,1)}, u32[]{:S(2)}) copy-start(bf16[96,8192]{1,0:T(8,128)(2,1)} %get-tuple-element.16) | copy-start | bytes 4718596
  112.5 2.0 %copy-start = (bf16[96,8192]{1,0:T(8,128)(2,1)S(1)}, bf16[96,8192]{1,0:T(8,128)(2,1)}, u32[]{:S(2)}) copy-start(bf16[96,8192]{1,0:T(8,128)(2,1)} %get-tuple-element.17) | copy-start | bytes 4718596

commit v3 on v2

--- a/solution.py
+++ b/solution.py
@@ -1,5 +1,3 @@
-import functools
-
 import jax
 import jax.numpy as jnp
 from jax import lax
@@ -91,8 +89,9 @@
     pl.semaphore_wait(pltpu.get_barrier_semaphore(), len(partners))
 
 
-def gather(g, cp, name, half, part, tick):
+def gather(g, cp, name, half, part):
     sib = {"tp": g.at(0, 0, True)}
+    dirs = (1, -1)
 
     def nbr(h, axis, d):
         return {"tp": g.block(h, d, 0) if axis == 1 else g.block(h, 0, d)}
@@ -107,12 +106,6 @@
         ref = half(g.block(h, o1, o2), h)
         cp.start((name, "s", h, o1, o2), ref, ref, sib)
 
-    def from_sib(h, o1, o2):
-        b = g.block(h, o1, o2, True)
-        cp.wait((name, "s", h, o1, o2), half(b, h), sib)
-        tick(b, h)
-
-    dirs = (1, -1)
     for h in (0, 1):
         for d in dirs:
             send(("p1", h, d), h, 1, d, half(g.tp, h))
@@ -121,10 +114,6 @@
             send(("p2", h, 0, d), h, 2, d, half(g.tp, h))
     for h in (0, 1):
         across(h, 0, 0)
-    yield
-    for h in (0, 1):
-        tick(g.tp, h)
-        from_sib(h, 0, 0)
     for d in dirs:
         for h in (0, 1):
             b = g.block(h, -d, 0)
@@ -133,17 +122,12 @@
             for e in dirs:
                 send(("p2", h, -d, e), h, 2, e, half(b, h))
             across(h, -d, 0)
-            tick(b, h)
-    yield
     for e in dirs:
         for h in (0, 1):
             b = g.block(h, 0, -e)
             got(("p2", h, 0, e), h, 2, -e, half(b, h))
             send(("f2", h, 0, e), h, 2, e, part(b, h, e, 0))
             across(h, 0, -e)
-            tick(b, h)
-            from_sib(h, -e, 0)
-    yield
     for h in (0, 1):
         b = g.block(h, 2, 0)
         for d in dirs:
@@ -151,10 +135,6 @@
         for e in dirs:
             send(("p2", h, 2, e), h, 2, e, half(b, h))
         across(h, 2, 0)
-        tick(b, h)
-        from_sib(h, 0, -1)
-        from_sib(h, 0, 1)
-    yield
     for o1 in (-1, 1):
         for e in dirs:
             for h in (0, 1):
@@ -162,50 +142,32 @@
                 got(("p2", h, o1, e), h, 2, -e, half(b, h))
                 send(("f2", h, o1, e), h, 2, e, part(b, h, e, o1))
                 across(h, o1, -e)
-                tick(b, h)
-                if (o1, e) == (-1, 1):
-                    from_sib(h, 2, 0)
-    yield
     for h in (0, 1):
         b = g.block(h, 0, 2)
         for e in dirs:
             got(("f2", h, 0, e), h, 2, -e, part(b, h, e, 0))
         across(h, 0, 2)
-        tick(b, h)
-        for o1 in (-1, 1):
-            for e in dirs:
-                from_sib(h, o1, -e)
-    yield
     for e in dirs:
         for h in (0, 1):
             b = g.block(h, 2, -e)
             got(("p2", h, 2, e), h, 2, -e, half(b, h))
             send(("f2", h, 2, e), h, 2, e, part(b, h, e, 2))
             across(h, 2, -e)
-            tick(b, h)
-            if e == 1:
-                from_sib(h, 0, 2)
-    yield
     for o1 in (-1, 1):
         for h in (0, 1):
             b = g.block(h, o1, 2)
             for e in dirs:
                 got(("f2", h, o1, e), h, 2, -e, part(b, h, e, o1))
             across(h, o1, 2)
-            tick(b, h)
-            from_sib(h, 2, -o1)
-    yield
     for h in (0, 1):
         b = g.block(h, 2, 2)
         for e in dirs:
             got(("f2", h, 2, e), h, 2, -e, part(b, h, e, 2))
         across(h, 2, 2)
-        tick(b, h)
-        from_sib(h, -1, 2)
-        from_sib(h, 1, 2)
-    for h in (0, 1):
-        from_sib(h, 2, 2)
-    yield
+    for h in (0, 1):
+        for o1 in (0, -1, 1, 2):
+            for o2 in (0, -1, 1, 2):
+                cp.wait((name, "s", h, o1, o2), half(g.block(h, o1, o2, True), h), sib)
 
 
 def column(row):
@@ -273,9 +235,10 @@
 
 def layer_kernel(
     tok_ref, cot_ref, ids_ref, w_ref, gw_hbm, uw_hbm, dw_hbm,
-    gate_ref, up_ref, down_ref, mixed_ref, gt_ref, gc_ref,
-    gw, uw, dw, gwt, uwt, dwt, pack, all_ref, win, hx, gy, uy,
-    full, part_ref, sib, chip, ra, rb, mid, fin, rows, got, rows2, got2, red, local, send, recv,
+    wide_ref, rows_ref, gc_ref,
+    gw, uw, dw, gwt, uwt, dwt, pack, all_ref, wx, wd, hx, gy, uy,
+    act, ship, relay, part_ref, sib, chip, far, tmp, near, mid, fin,
+    rows, got, rows2, got2, red, local, send, recv,
 ):
     g = Grid()
     cp = Copies(send, recv)
@@ -319,18 +282,8 @@
 
     lax.fori_loop(0, gw.shape[0] // 256, turn, 0)
     from_all_groups(g, cp, got, "out")
-    own = dot(got[...], pack[...], 0, 0)
-    all_ref[pl.ds(pl.multiple_of(g.tp * width, width), width), :] = own.astype(BF16)
-    low = iota((width, 128), 1) < 64
-    o = [own[:, i * 128 : (i + 1) * 128] for i in range(5)]
-    x2 = jnp.where(low, o[2], 0.0)
-    d2 = jnp.where(low, turned(o[2]), 0.0)
-    for i, t in enumerate((turned(x2), o[0], o[1])):
-        win[0, :, i * 128 : (i + 1) * 128] = t.astype(BF16)
-    for i, t in enumerate((o[0], o[1], x2)):
-        win[1, :, i * 128 : (i + 1) * 128] = t.astype(BF16)
-    for i, t in enumerate((o[3], o[4], d2)):
-        win[2, :, i * 128 : (i + 1) * 128] = t.astype(BF16)
+    own = dot(got[...], pack[...], 0, 0).astype(BF16)
+    all_ref[pl.ds(pl.multiple_of(g.tp * width, width), width), :] = own
     half_w = width // 2
 
     def half_in(b, h):
@@ -340,18 +293,16 @@
         rng = pl.ds(0, 384) if (q > 0) == (o in (0, 1)) else pl.ds(384, 256)
         return all_ref.at[pl.ds(pl.multiple_of(b * width + h * half_w, 16), half_w), rng]
 
-    for _ in gather(g, cp, "in", half_in, part_in, lambda b, h: None):
-        pass
+    gather(g, cp, "in", half_in, part_in)
 
     hh = size // 2
-    mine = g.tp * size
 
     def units(h, _):
         r = pl.ds(pl.multiple_of(h * hh, hh), hh)
         gate = dot(gwt[r, :], all_ref[:, :WIN], 1, 0)
         upp = dot(uwt[r, :], all_ref[:, :WIN], 1, 0)
         gh = dot(dw[r, :], all_ref[:, 256:], 1, 0)
-        at = pl.ds(pl.multiple_of(mine + h * hh, hh), hh)
+        place = jnp.where(h == 0, g.x, g.y)
         lo = iota((hh, 128), 1) < 64
         for i in range(3):
             t = slice(i * 128, (i + 1) * 128)
@@ -364,36 +315,96 @@
             gu = d * active
             if i == 2:
                 hid, gg, gu = (jnp.where(lo, a, 0.0) for a in (hid, gg, gu))
-                full[at, 256:384] = (hid + turned(gg)).astype(BF16)
+                act[h, place, g.c, :, 256:384] = (gg + turned(hid)).astype(BF16)
                 gy[r, 0:128] = turned(gg).astype(BF16)
                 uy[r, 0:128] = turned(gu).astype(BF16)
             else:
-                full[at, t] = hid.astype(BF16)
-                full[at, 384 + i * 128 : 512 + i * 128] = gg.astype(BF16)
+                act[h, place, g.c, :, t] = gg.astype(BF16)
+                act[h, place, g.c, :, 384 + i * 128 : 512 + i * 128] = hid.astype(BF16)
                 gy[r, (i + 1) * 128 : (i + 2) * 128] = gg.astype(BF16)
                 uy[r, (i + 1) * 128 : (i + 2) * 128] = gu.astype(BF16)
             hx[r, t] = hid.astype(BF16)
-            full[at, 640 + i * 128 : 768 + i * 128] = gu.astype(BF16)
+            act[h, place, g.c, :, 640 + i * 128 : 768 + i * 128] = gu.astype(BF16)
         return _
 
     lax.fori_loop(0, 2, units, 0)
 
-    def half(b, h):
-        return full.at[pl.ds(pl.multiple_of(b * size + h * hh, 64), hh)]
-
-    def part(b, h, q, o):
-        off = 0 if q > 0 else hh // 2
-        return full.at[pl.ds(pl.multiple_of(b * size + h * hh + off, 64), hh // 2)]
-
-    def tick(b, h):
-        at = pl.multiple_of(b * size + h * hh, 128)
-        blk = full[pl.ds(at, hh), :]
-        gate_ref[:, pl.ds(at, hh)] = dot(win[0], blk[:, 256:640], 1, 1).astype(BF16)
-        up_ref[:, pl.ds(at, hh)] = dot(win[1], blk[:, 640:], 1, 1).astype(BF16)
-        down_ref[:, pl.ds(at, hh)] = dot(win[2], blk[:, :WIN], 1, 1).astype(BF16)
-
-    steps = gather(g, cp, "act", half, part, tick)
-    next(steps)
+    dirs = (1, -1)
+    dests = (0, 1, -1, 2)
+    lines = (0, -1, 1, 2)
+
+    def spot(h, o1):
+        return ((g.x if h == 0 else g.y) + (o1 + SIDE)) % SIDE
+
+    def nbr(h, axis, d):
+        return {"tp": g.block(h, d, 0) if axis == 1 else g.block(h, 0, d)}
+
+    def piece(h, o1, d):
+        return act.at[h, spot(h, o1), g.c, pl.ds(0 if d > 0 else hh // 2, hh // 2)]
+
+    def cross(h, o1):
+        ref = act.at[h, spot(h, o1), g.c]
+        cp.start(("s", h, o1), ref, ref, sib_dev)
+
+    def crossed(h, o1):
+        cp.wait(("s", h, o1), act.at[h, spot(h, o1), 1 - g.c], sib_dev)
+
+    def columns(h, o1, o2, k):
+        b = g.block(h, o1, o2, k == 1)
+        return pl.ds(pl.multiple_of(b * size + h * hh, 128), hh)
+
+    def make(h, o1, k):
+        j = lines.index(o1)
+        c = g.c if k == 0 else 1 - g.c
+        blk = act[h, spot(h, o1), c]
+        for i, (left, right) in enumerate(
+            ((wx[h], blk[:, :WIN]), (wx[h], blk[:, 640:]), (wd[h], blk[:, 256:640]))
+        ):
+            res = dot(left, right, 1, 1).astype(BF16)
+            wide_ref[i, :, columns(h, o1, 0, k)] = res[0:width]
+            for n in range(3):
+                ship[h, j, k, n, i] = res[(n + 1) * width : (n + 2) * width]
+        for n, d in enumerate(dirs):
+            cp.start(
+                ("w", h, o1, k, d), ship.at[h, j, k, n], wide_ref.at[:, :, columns(h, o1, 0, k)], nbr(h, 2, d)
+            )
+        d = dirs[k]
+        cp.start(("v", h, o1, d), ship.at[h, j, k, 2], relay.at[h, j, k], nbr(h, 2, d))
+
+    def pass_on(h, o1):
+        j = lines.index(o1)
+        for k, d in enumerate(dirs):
+            cp.wait(("v", h, o1, d), relay.at[h, j, k], nbr(h, 2, -d))
+            cp.start(
+                ("u", h, o1, d), relay.at[h, j, k], wide_ref.at[:, :, columns(h, o1, -d, k)], nbr(h, 2, d)
+            )
+
+    def landed(h, o1):
+        for k, d in enumerate(dirs):
+            for e in dirs:
+                cp.wait(("w", h, o1, k, e), wide_ref.at[:, :, columns(h, o1, -e, k)], nbr(h, 2, -e))
+            cp.wait(("u", h, o1, d), wide_ref.at[:, :, columns(h, o1, 2, k)], nbr(h, 2, -d))
+
+    for h in (0, 1):
+        ref = act.at[h, spot(h, 0), g.c]
+        for d in dirs:
+            cp.start(("p", h, d), ref, ref, nbr(h, 1, d))
+        cross(h, 0)
+    low = iota((width, 128), 1) < 64
+    for h in (0, 1):
+        for n, o2 in enumerate(dests):
+            at = pl.ds(pl.multiple_of(g.block(h, 0, o2) * width, width), width)
+            r = pl.ds(n * width, width)
+            shared = all_ref[at, 256:384].astype(F32)
+            wx[h, r, 0:256] = all_ref[at, 0:256]
+            wx[h, r, 256:384] = jnp.where(low, shared, 0.0).astype(BF16)
+            wd[h, r, 0:128] = jnp.where(low, 0.0, shared).astype(BF16)
+            wd[h, r, 128:384] = all_ref[at, 384:640]
+    for h in (0, 1):
+        make(h, 0, 0)
+    for h in (0, 1):
+        crossed(h, 0)
+        make(h, 0, 1)
 
     def partial(c):
         def one(i, _):
@@ -413,7 +424,7 @@
     cp.wait("pair", sib, sib_dev)
 
     def add_pair(i, _):
-        chip[i] = (part_ref[g.c, i].astype(F32) + sib[i].astype(F32)).astype(BF16)
+        chip[i // SIDE, i % SIDE] = (part_ref[g.c, i].astype(F32) + sib[i].astype(F32)).astype(BF16)
         return _
 
     lax.fori_loop(0, SIDE * SIDE, add_pair, 0)
@@ -424,34 +435,47 @@
     def x_of(d):
         return (g.x + d + SIDE) % SIDE
 
-    lo, hi = pl.ds(0, half_w), pl.ds(half_w, half_w)
-    for i, d in enumerate((1, -1, 2)):
-        cp.start(("a1", d), chip.at[pl.ds(y_of(d) * SIDE, SIDE), lo], ra.at[i], {"tp": g.at(d, 0)})
-        for r in range(SIDE):
-            cp.start(("b1", d, r), chip.at[r * SIDE + x_of(d), hi], rb.at[i, r], {"tp": g.at(0, d)})
-    next(steps)
-    for i, d in enumerate((1, -1, 2)):
-        cp.wait(("a1", d), ra.at[i], {"tp": g.at(-d, 0)})
-        for r in range(SIDE):
-            cp.wait(("b1", d, r), rb.at[i, r], {"tp": g.at(0, -d)})
-
-    def add_a(r, _):
-        s = chip[g.y * SIDE + r, lo, :].astype(F32)
-        for i in range(3):
-            s = s + ra[i, r].astype(F32)
-        mid[0, r] = s.astype(BF16)
-        s = chip[r * SIDE + g.x, hi, :].astype(F32)
-        for i in range(3):
-            s = s + rb[i, r].astype(F32)
-        mid[1, r] = s.astype(BF16)
-        return _
-
-    lax.fori_loop(0, SIDE, add_a, 0)
+    rng = (pl.ds(0, half_w), pl.ds(half_w, half_w))
+
+    def share(h, d, q):
+        two = pl.ds(2 * q, 2)
+        return (y_of(d), two, rng[0]) if h == 0 else (two, x_of(d), rng[1])
+
+    for h in (0, 1):
+        for q, d in enumerate(dirs):
+            cp.start(("r1", h, d), chip.at[share(h, 2, q)], far.at[h, q], nbr(h, 2, d))
+        for q, d in enumerate(dirs):
+            cp.start(("r2", h, d), chip.at[share(h, d, 1 - q)], near.at[h, q, 1], nbr(h, 2, d))
+    for q, d in enumerate(dirs):
+        for h in (0, 1):
+            cp.wait(("r1", h, d), far.at[h, q], nbr(h, 2, -d))
+            tmp[h, q] = (chip[share(h, d, q)].astype(F32) + far[h, q].astype(F32)).astype(BF16)
+            cp.start(("r3", h, d), tmp.at[h, q], near.at[h, q, 0], nbr(h, 2, d))
+    for d in dirs:
+        for h in (0, 1):
+            cp.wait(("p", h, d), act.at[h, spot(h, -d), g.c], nbr(h, 1, -d))
+            cp.start(("f", h, d), piece(h, -d, d), piece(h, -d, d), nbr(h, 1, d))
+            cross(h, -d)
+    for h in (0, 1):
+        pass_on(h, 0)
+    for d in dirs:
+        for h in (0, 1):
+            make(h, -d, 0)
+    for h in (0, 1):
+        for q, d in enumerate(dirs):
+            cp.wait(("r2", h, d), near.at[h, q, 1], nbr(h, 2, -d))
+            cp.wait(("r3", h, d), near.at[h, q, 0], nbr(h, 2, -d))
+        for q in (0, 1):
+            t = chip[share(h, 0, q)].astype(F32)
+            t = t + near[h, q, 0].astype(F32) + near[h, 1 - q, 1].astype(F32)
+            mid[h, 2 * q : 2 * q + 2] = t.astype(BF16)
     for i, d in enumerate((1, -1, 2)):
         cp.start(("a2", d), mid.at[0, x_of(d)], fin.at[0, i], {"tp": g.at(0, d)})
         cp.start(("b2", d), mid.at[1, y_of(d)], fin.at[1, i], {"tp": g.at(d, 0)})
-    next(steps)
-    next(steps)
+    for d in dirs:
+        for h in (0, 1):
+            crossed(h, -d)
+            make(h, -d, 1)
     for i, d in enumerate((1, -1, 2)):
         cp.wait(("a2", d), fin.at[0, i], {"tp": g.at(0, -d)})
         cp.wait(("b2", d), fin.at[1, i], {"tp": g.at(-d, 0)})
@@ -465,57 +489,66 @@
     rows2[...] = dot(pack[...], total, 1, 1).astype(BF16)
     to_all_groups(g, cp, rows2, got2, "back")
     own_group(g, rows2, got2)
-    next(steps)
+    for h in (0, 1):
+        for d in dirs:
+            cp.wait(("f", h, d), piece(h, 2, d), nbr(h, 1, -d))
+        cross(h, 2)
+        make(h, 2, 0)
+    for h in (0, 1):
+        crossed(h, 2)
+        make(h, 2, 1)
+        for o1 in (-1, 1):
+            pass_on(h, o1)
     from_all_groups(g, cp, got2, "back")
     back = got2[...]
     outs = [dot(first[k], back, 1, 0) for k in (0, 1)]
-    mixed_ref[...] = (w[0] * outs[0] + w[1] * outs[1]).astype(BF16)
-    gt_ref[...] = (dot(second[0], back, 1, 0) + dot(second[1], back, 1, 0)).astype(BF16)
+    rows_ref[0] = (w[0] * outs[0] + w[1] * outs[1]).astype(BF16)
+    rows_ref[1] = (dot(second[0], back, 1, 0) + dot(second[1], back, 1, 0)).astype(BF16)
     inner = [as_row(jnp.sum(cot * outs[k], axis=1, keepdims=True)) for k in (0, 1)]
     sub = iota((8, width), 0)
     red[0] = jnp.zeros((8, 128), F32)
     red[0, :, 0:width] = jnp.where(sub == 0, inner[0], jnp.where(sub == 1, inner[1], 0.0))
     cp.start("g0", red.at[0], red.at[1], sib_dev)
-    next(steps)
+    for h in (0, 1):
+        pass_on(h, 2)
     cp.wait("g0", red.at[1], sib_dev)
     red[2 + g.x] = red[0] + red[1]
     for d in (1, -1, 2):
         cp.start(("g1", d), red.at[2 + g.x], red.at[2 + g.x], {"tp": g.at(0, d)})
-    next(steps)
+    for h in (0, 1):
+        landed(h, 0)
     for d in (1, -1, 2):
         cp.wait(("g1", d), red.at[2 + x_of(-d)], {"tp": g.at(0, -d)})
     red[6 + g.y] = (red[2] + red[3]) + (red[4] + red[5])
     for d in (1, -1, 2):
         cp.start(("g2", d), red.at[6 + g.y], red.at[6 + g.y], {"tp": g.at(d, 0)})
-    for _ in steps:
-        pass
+    for h in (0, 1):
+        for o1 in (-1, 1, 2):
+            landed(h, o1)
     for d in (1, -1, 2):
         cp.wait(("g2", d), red.at[6 + y_of(-d)], {"tp": g.at(-d, 0)})
     gc_ref[...] = ((red[6] + red[7]) + (red[8] + red[9]))[0:2, 0:width]
     cp.finish()
 
 
-N_COPIES = 2 * 7 + 2 * (40 + 32) + 1 + 15 + 6 + 7
+N_COPIES = 2 * 7 + (40 + 32) + (4 + 4 + 8 + 32 + 16 + 16) + 1 + 12 + 6 + 7
 
 
 def layer(tokens, cotangent, ids, weights, gate_w, up_w, down_w):
     width = tokens.shape[1]
     model, size = gate_w.shape
     n = model // width
-    wide = jax.ShapeDtypeStruct((width, n * size), BF16)
     ANY = pl.BlockSpec(memory_space=pl.ANY)
+    half_w = width // 2
     return pl.pallas_call(
         layer_kernel,
         out_shape=(
-            wide,
-            wide,
-            wide,
-            jax.ShapeDtypeStruct(cotangent.shape, BF16),
-            jax.ShapeDtypeStruct(cotangent.shape, BF16),
-            jax.ShapeDtypeStruct(ids.shape, F32),
+            pltpu.VMEM((3, width, n * size), BF16),
+                        pltpu.VMEM((2, *cotangent.shape), BF16),
+            pltpu.VMEM(ids.shape, F32),
         ),
         in_specs=[VMEM] * 4 + [ANY] * 3,
-        out_specs=(VMEM,) * 6,
+        out_specs=(VMEM,) * 3,
         scratch_shapes=[
             pltpu.VMEM((model, size), BF16),
             pltpu.VMEM((model, size), BF16),
@@ -525,18 +558,22 @@
             pltpu.VMEM((model, size), BF16),
             pltpu.VMEM((ROWS, PACK), BF16),
             pltpu.VMEM((model, PACK), BF16),
-            pltpu.VMEM((3, width, WIN), BF16),
+            pltpu.VMEM((2, SIDE * width, WIN), BF16),
+            pltpu.VMEM((2, SIDE * width, WIN), BF16),
             pltpu.VMEM((size, WIN), BF16),
             pltpu.VMEM((size, WIN), BF16),
             pltpu.VMEM((size, WIN), BF16),
-            pltpu.VMEM((n * size, 1024), BF16),
+            pltpu.VMEM((2, SIDE, 2, size // 2, 1024), BF16),
+            pltpu.VMEM((2, SIDE, 2, 3, 3, width, size // 2), BF16),
+            pltpu.VMEM((2, SIDE, 2, 3, width, size // 2), BF16),
             pltpu.VMEM((2, SIDE * SIDE, width, PACK), BF16),
             pltpu.VMEM((SIDE * SIDE, width, PACK), BF16),
-            pltpu.VMEM((SIDE * SIDE, width, PACK), BF16),
-            pltpu.VMEM((3, SIDE, width // 2, PACK), BF16),
-            pltpu.VMEM((3, SIDE, width // 2, PACK), BF16),
-            pltpu.VMEM((2, SIDE, width // 2, PACK), BF16),
-            pltpu.VMEM((2, 3, width // 2, PACK), BF16),
+            pltpu.VMEM((SIDE, SIDE, width, PACK), BF16),
+            pltpu.VMEM((2, 2, 2, half_w, PACK), BF16),
+            pltpu.VMEM((2, 2, 2, half_w, PACK), BF16),
+            pltpu.VMEM((2, 2, 2, 2, half_w, PACK), BF16),
+            pltpu.VMEM((2, SIDE, half_w, PACK), BF16),
+            pltpu.VMEM((2, 3, half_w, PACK), BF16),
             pltpu.VMEM((ROWS, width), BF16),
             pltpu.VMEM((ROWS, width), BF16),
             pltpu.VMEM((ROWS, width), BF16),
@@ -547,17 +584,17 @@
             pltpu.SemaphoreType.DMA((N_COPIES,)),
         ],
         compiler_params=pltpu.CompilerParams(
-            collective_id=0, has_side_effects=True, vmem_limit_bytes=63 * 2**20
+            collective_id=0, has_side_effects=True, vmem_limit_bytes=52 * 2**20
         ),
         name="layer",
     )(tokens, cotangent, ids, weights, gate_w, up_w, down_w)
 
 
 def body(tokens, cotangent, expert_ids, combine_weights, w_gate, w_up, w_down):
-    gate, up, down, mixed, gt, gc = layer(
+    wide, back, gc = layer(
         tokens, cotangent, expert_ids.T, combine_weights.T, w_gate[0], w_up[0], w_down[0]
     )
-    return mixed, gt, gc.T, gate[None], up[None], down.T[None]
+    return back[0], back[1], gc.T, wide[0][None], wide[1][None], wide[2].T[None]
 
 
 def solution(mesh):

time: 116 us -> 96.8 us (0.83)
  Pallas kernels: 105 us -> 92.1 us
  local copies, waits for them, and re-layouts: 9.81 us -> 3.46 us
    pallas_call x1, Pallas kernels: 105 us -> 92.1 us  [layer(): pl.pallas_call(layer_kernel, out_shape=(pltpu.VMEM((3, width, n * size),...]
    unnamed x10 -> x1, local copies, waits for them, and re-layouts: 9.81 us -> 0.56 us
    broadcast_in_dim x0 -> x1, local copies, waits for them, and re-layouts: none -> 2.28 us  [body(): wide[2].T[None]]
where the time goes in v3:
time: 96.8 us; the launch traced here: 96.2 us
  Pallas kernels  92.1 us (95%)
  local copies, waits for them, and re-layouts  3.46 us (4%)
    pallas_call x1, Pallas kernels, layer(): pl.pallas_call(layer_kernel, out_shape=(pltpu.VMEM((3, width, n * size),...  92.1 us
    broadcast_in_dim x1, local copies, waits for them, and re-layouts, body(): wide[2].T[None]  2.28 us

profile of v3, /device:TPU:1, one launch (start us, length us, event | category | flops | bytes accessed | tf_op | source)
XLA Modules:
  0.0 96.2 jit_solution(6168567106203420078)
XLA Ops:
  0.6 92.1 %layer.1 = (bf16[3,96,8192]{2,1,0:T(8,128)(2,1)S(1)}, bf16[2,96,96]{2,1,0:T(8,128)(2,1)S(1)}, f32[2,96]{1,0:T(2,128)S(1)}) custom-call(bf16[96,96]{1,0:T(8,128)(2,1)} %tok_ref.1, bf16[96,96]{1,0:T(8,128)(2,1)} %cot_ref.1, s32[2,96]{1,0:T(2,128)} %bitcast.20, f32[2,96]{1,0:T(2,128)} %bitcast.21, bf16[3072,256]{1,0:T(8,128)(2,1)} %bitcast.17, ...), custom_call_target="tpu_custom_call" | custom-call | tf_op jit(solution)/shard_map/layer/pallas_call | solution.py:543
  92.7 0.6 copy.14
  93.3 0.6 slice_bitcast_fusion.1
  93.9 2.3 %slice_bitcast_fusion = (bf16[1,8192,96]{1,2,0:T(8,128)(2,1)}, bf16[1,96,8192]{2,1,0:T(8,128)(2,1)}, bf16[1,96,8192]{2,1,0:T(8,128)(2,1)}) fusion(bf16[3,96,8192]{2,1,0:T(8,128)(2,1)S(1)} %get-tuple-element.11), kind=kLoop, calls=%fused_computation | loop fusion | bytes 9437184 | tf_op jit(solution)/shard_map/broadcast_in_dim | solution.py:597

commit v4 on v3

--- a/solution.py
+++ b/solution.py
@@ -107,7 +107,7 @@
         cp.start((name, "s", h, o1, o2), ref, ref, sib)
 
     for h in (0, 1):
-        for d in dirs:
+        for d in dirs + (2,):
             send(("p1", h, d), h, 1, d, half(g.tp, h))
     for h in (0, 1):
         for d in dirs:
@@ -118,23 +118,21 @@
         for h in (0, 1):
             b = g.block(h, -d, 0)
             got(("p1", h, d), h, 1, -d, half(b, h))
-            send(("f1", h, d), h, 1, d, part(b, h, d, 0))
             for e in dirs:
                 send(("p2", h, -d, e), h, 2, e, half(b, h))
             across(h, -d, 0)
+    for h in (0, 1):
+        b = g.block(h, 2, 0)
+        got(("p1", h, 2), h, 1, 2, half(b, h))
+        for e in dirs + (2,):
+            send(("p2", h, 2, e), h, 2, e, half(b, h))
+        across(h, 2, 0)
     for e in dirs:
         for h in (0, 1):
             b = g.block(h, 0, -e)
             got(("p2", h, 0, e), h, 2, -e, half(b, h))
             send(("f2", h, 0, e), h, 2, e, part(b, h, e, 0))
             across(h, 0, -e)
-    for h in (0, 1):
-        b = g.block(h, 2, 0)
-        for d in dirs:
-            got(("f1", h, d), h, 1, -d, part(b, h, d, 0))
-        for e in dirs:
-            send(("p2", h, 2, e), h, 2, e, half(b, h))
-        across(h, 2, 0)
     for o1 in (-1, 1):
         for e in dirs:
             for h in (0, 1):
@@ -151,7 +149,6 @@
         for h in (0, 1):
             b = g.block(h, 2, -e)
             got(("p2", h, 2, e), h, 2, -e, half(b, h))
-            send(("f2", h, 2, e), h, 2, e, part(b, h, e, 2))
             across(h, 2, -e)
     for o1 in (-1, 1):
         for h in (0, 1):
@@ -161,8 +158,7 @@
             across(h, o1, 2)
     for h in (0, 1):
         b = g.block(h, 2, 2)
-        for e in dirs:
-            got(("f2", h, 2, e), h, 2, -e, part(b, h, e, 2))
+        got(("p2", h, 2, 2), h, 2, 2, half(b, h))
         across(h, 2, 2)
     for h in (0, 1):
         for o1 in (0, -1, 1, 2):
@@ -234,8 +230,9 @@
 
 
 def layer_kernel(
-    tok_ref, cot_ref, ids_ref, w_ref, gw_hbm, uw_hbm, dw_hbm,
+    tok_hbm, cot_hbm, ids_hbm, w_hbm, gw_hbm, uw_hbm, dw_hbm,
     wide_ref, rows_ref, gc_ref,
+    tok_ref, cot_ref, ids_ref, w_ref,
     gw, uw, dw, gwt, uwt, dwt, pack, all_ref, wx, wd, hx, gy, uy,
     act, ship, relay, part_ref, sib, chip, far, tmp, near, mid, fin,
     rows, got, rows2, got2, red, local, send, recv,
@@ -244,16 +241,29 @@
     cp = Copies(send, recv)
     sib_dev = {"tp": g.at(0, 0, True)}
     ring = ((0, 1), (0, -1), (0, 2), (1, 0), (-1, 0), (2, 0))
+    others = ((0, 1, True), (0, -1, True), (0, 2, True))
     partners = (
-        [sib_dev] + [{"tp": g.at(*o)} for o in ring] + [{"ep": g.up(k)} for k in range(1, GROUPS)]
+        [sib_dev] + [{"tp": g.at(*o)} for o in ring + others] + [{"ep": g.up(k)} for k in range(1, GROUPS)]
     )
     greet(partners)
     loads = [
         pltpu.make_async_copy(a, b, local.at[i])
-        for i, (a, b) in enumerate(((gw_hbm, gw), (uw_hbm, uw), (dw_hbm, dw)))
+        for i, (a, b) in enumerate(
+            (
+                (tok_hbm, tok_ref),
+                (cot_hbm, cot_ref),
+                (ids_hbm, ids_ref),
+                (w_hbm, w_ref),
+                (gw_hbm, gw),
+                (uw_hbm, uw),
+                (dw_hbm, dw),
+            )
+        )
     ]
     for c in loads:
         c.start()
+    for c in loads[:4]:
+        c.wait()
 
     width = tok_ref.shape[1]
     ids = [column(ids_ref[k : k + 1, :].astype(F32)) for k in (0, 1)]
@@ -268,7 +278,7 @@
     to_all_groups(g, cp, rows, got, "out")
     own_group(g, rows, got)
     fill_packing(pack)
-    for c in loads:
+    for c in loads[4:]:
         c.wait()
     size = gw.shape[1]
     blocks = gw.shape[0] // width
@@ -298,11 +308,11 @@
     hh = size // 2
 
     def units(h, _):
-        r = pl.ds(pl.multiple_of(h * hh, hh), hh)
+        r = pl.ds(h * hh, hh)
         gate = dot(gwt[r, :], all_ref[:, :WIN], 1, 0)
         upp = dot(uwt[r, :], all_ref[:, :WIN], 1, 0)
         gh = dot(dw[r, :], all_ref[:, 256:], 1, 0)
-        place = jnp.where(h == 0, g.x, g.y)
+        place = g.x if h == 0 else g.y
         lo = iota((hh, 128), 1) < 64
         for i in range(3):
             t = slice(i * 128, (i + 1) * 128)
@@ -327,7 +337,6 @@
             act[h, place, g.c, :, 640 + i * 128 : 768 + i * 128] = gu.astype(BF16)
         return _
 
-    lax.fori_loop(0, 2, units, 0)
 
     dirs = (1, -1)
     dests = (0, 1, -1, 2)
@@ -386,6 +395,7 @@
             cp.wait(("u", h, o1, d), wide_ref.at[:, :, columns(h, o1, 2, k)], nbr(h, 2, -d))
 
     for h in (0, 1):
+        units(h, 0)
         ref = act.at[h, spot(h, 0), g.c]
         for d in dirs:
             cp.start(("p", h, d), ref, ref, nbr(h, 1, d))
@@ -476,6 +486,14 @@
         for h in (0, 1):
             crossed(h, -d)
             make(h, -d, 1)
+    for h in (0, 1):
+        for d in dirs:
+            cp.wait(("f", h, d), piece(h, 2, d), nbr(h, 1, -d))
+        cross(h, 2)
+        make(h, 2, 0)
+    for h in (0, 1):
+        crossed(h, 2)
+        make(h, 2, 1)
     for i, d in enumerate((1, -1, 2)):
         cp.wait(("a2", d), fin.at[0, i], {"tp": g.at(0, -d)})
         cp.wait(("b2", d), fin.at[1, i], {"tp": g.at(-d, 0)})
@@ -490,13 +508,6 @@
     to_all_groups(g, cp, rows2, got2, "back")
     own_group(g, rows2, got2)
     for h in (0, 1):
-        for d in dirs:
-            cp.wait(("f", h, d), piece(h, 2, d), nbr(h, 1, -d))
-        cross(h, 2)
-        make(h, 2, 0)
-    for h in (0, 1):
-        crossed(h, 2)
-        make(h, 2, 1)
         for o1 in (-1, 1):
             pass_on(h, o1)
     from_all_groups(g, cp, got2, "back")
@@ -506,32 +517,33 @@
     rows_ref[1] = (dot(second[0], back, 1, 0) + dot(second[1], back, 1, 0)).astype(BF16)
     inner = [as_row(jnp.sum(cot * outs[k], axis=1, keepdims=True)) for k in (0, 1)]
     sub = iota((8, width), 0)
-    red[0] = jnp.zeros((8, 128), F32)
-    red[0, :, 0:width] = jnp.where(sub == 0, inner[0], jnp.where(sub == 1, inner[1], 0.0))
-    cp.start("g0", red.at[0], red.at[1], sib_dev)
+    red[2 * g.x + g.c] = jnp.zeros((8, 128), F32)
+    red[2 * g.x + g.c, :, 0:width] = jnp.where(sub == 0, inner[0], jnp.where(sub == 1, inner[1], 0.0))
+    slot = red.at[2 * g.x + g.c]
+    for d in (0, 1, -1, 2):
+        for k in (0, 1):
+            if d or k:
+                cp.start(("g1", d, k), slot, slot, {"tp": g.at(0, d, k == 1)})
     for h in (0, 1):
         pass_on(h, 2)
-    cp.wait("g0", red.at[1], sib_dev)
-    red[2 + g.x] = red[0] + red[1]
+    for d in (0, 1, -1, 2):
+        for k in (0, 1):
+            if d or k:
+                c = 1 - g.c if k else g.c
+                cp.wait(("g1", d, k), red.at[2 * x_of(-d) + c], {"tp": g.at(0, -d, k == 1)})
+    red[8 + g.y] = ((red[0] + red[1]) + (red[2] + red[3])) + ((red[4] + red[5]) + (red[6] + red[7]))
     for d in (1, -1, 2):
-        cp.start(("g1", d), red.at[2 + g.x], red.at[2 + g.x], {"tp": g.at(0, d)})
-    for h in (0, 1):
-        landed(h, 0)
-    for d in (1, -1, 2):
-        cp.wait(("g1", d), red.at[2 + x_of(-d)], {"tp": g.at(0, -d)})
-    red[6 + g.y] = (red[2] + red[3]) + (red[4] + red[5])
-    for d in (1, -1, 2):
-        cp.start(("g2", d), red.at[6 + g.y], red.at[6 + g.y], {"tp": g.at(d, 0)})
-    for h in (0, 1):
-        for o1 in (-1, 1, 2):
+        cp.start(("g2", d), red.at[8 + g.y], red.at[8 + g.y], {"tp": g.at(d, 0)})
+    for h in (0, 1):
+        for o1 in (0, -1, 1, 2):
             landed(h, o1)
     for d in (1, -1, 2):
-        cp.wait(("g2", d), red.at[6 + y_of(-d)], {"tp": g.at(-d, 0)})
-    gc_ref[...] = ((red[6] + red[7]) + (red[8] + red[9]))[0:2, 0:width]
+        cp.wait(("g2", d), red.at[8 + y_of(-d)], {"tp": g.at(-d, 0)})
+    gc_ref[...] = ((red[8] + red[9]) + (red[10] + red[11]))[0:2, 0:width]
     cp.finish()
 
 
-N_COPIES = 2 * 7 + (40 + 32) + (4 + 4 + 8 + 32 + 16 + 16) + 1 + 12 + 6 + 7
+N_COPIES = 2 * 7 + (36 + 32) + (4 + 4 + 8 + 32 + 16 + 16) + 1 + 12 + 6 + 10
 
 
 def layer(tokens, cotangent, ids, weights, gate_w, up_w, down_w):
@@ -547,9 +559,13 @@
                         pltpu.VMEM((2, *cotangent.shape), BF16),
             pltpu.VMEM(ids.shape, F32),
         ),
-        in_specs=[VMEM] * 4 + [ANY] * 3,
+        in_specs=[ANY] * 7,
         out_specs=(VMEM,) * 3,
         scratch_shapes=[
+            pltpu.VMEM(tokens.shape, BF16),
+            pltpu.VMEM(tokens.shape, BF16),
+            pltpu.VMEM(ids.shape, jnp.int32),
+            pltpu.VMEM(ids.shape, F32),
             pltpu.VMEM((model, size), BF16),
             pltpu.VMEM((model, size), BF16),
             pltpu.VMEM((size, model), BF16),
@@ -578,8 +594,8 @@
             pltpu.VMEM((ROWS, width), BF16),
             pltpu.VMEM((ROWS, width), BF16),
             pltpu.VMEM((ROWS, width), BF16),
-            pltpu.VMEM((10, 8, 128), F32),
-            pltpu.SemaphoreType.DMA((3,)),
+            pltpu.VMEM((12, 8, 128), F32),
+            pltpu.SemaphoreType.DMA((7,)),
             pltpu.SemaphoreType.DMA((N_COPIES,)),
             pltpu.SemaphoreType.DMA((N_COPIES,)),
         ],
@@ -590,11 +606,35 @@
     )(tokens, cotangent, ids, weights, gate_w, up_w, down_w)
 
 
+def out_kernel(wide, rows, gc, mixed, gt, gco, gate, up, down, sem):
+    pairs = ((wide.at[0], gate), (wide.at[1], up), (wide.at[2], down), (rows.at[0], mixed), (rows.at[1], gt), (gc, gco))
+    copies = [pltpu.make_async_copy(a, b, sem.at[i]) for i, (a, b) in enumerate(pairs)]
+    for c in copies:
+        c.start()
+    for c in copies:
+        c.wait()
+
+
+def results(wide, rows, gc):
+    shapes = [rows.shape[1:]] * 2 + [gc.shape] + [wide.shape[1:]] * 3
+    types = [BF16, BF16, F32, BF16, BF16, BF16]
+    return pl.pallas_call(
+        out_kernel,
+        out_shape=tuple(jax.ShapeDtypeStruct(a, t) for a, t in zip(shapes, types)),
+        in_specs=[VMEM] * 3,
+        out_specs=(pl.BlockSpec(memory_space=pl.ANY),) * 6,
+        scratch_shapes=[pltpu.SemaphoreType.DMA((6,))],
+        compiler_params=pltpu.CompilerParams(vmem_limit_bytes=8 * 2**20),
+        name="results",
+    )(wide, rows, gc)
+
+
 def body(tokens, cotangent, expert_ids, combine_weights, w_gate, w_up, w_down):
     wide, back, gc = layer(
         tokens, cotangent, expert_ids.T, combine_weights.T, w_gate[0], w_up[0], w_down[0]
     )
-    return back[0], back[1], gc.T, wide[0][None], wide[1][None], wide[2].T[None]
+    mixed, gt, gc, gate, up, down = results(wide, back, gc)
+    return mixed, gt, gc.T, gate[None], up[None], down.T[None]
 
 
 def solution(mesh):

time: 96.8 us -> 90.4 us (0.934)
  local copies, waits for them, and re-layouts: 3.46 us -> 0 us
  Pallas kernels: 92.1 us -> 89.6 us
    pallas_call x1, Pallas kernels: 92.1 us -> 87.4 us  [layer(): pl.pallas_call(layer_kernel, out_shape=(pltpu.VMEM((3, width, n * size),...]
    broadcast_in_dim x1 -> x0, local copies, waits for them, and re-layouts: 2.28 us -> none  [body(): wide[2].T[None]]
    pallas_call x0 -> x1, Pallas kernels: none -> 2.24 us  [results(): pl.pallas_call(out_kernel, out_shape=tuple((jax.ShapeDtypeStruct(a, t) fo...]
where the time goes in v4:
time: 90.4 us; the launch traced here: 90.3 us
  Pallas kernels  89.6 us (99%)
    pallas_call x1, Pallas kernels, layer(): pl.pallas_call(layer_kernel, out_shape=(pltpu.VMEM((3, width, n * size),...  87.4 us
    pallas_call x1, Pallas kernels, results(): pl.pallas_call(out_kernel, out_shape=tuple((jax.ShapeDtypeStruct(a, t) fo...  2.24 us

profile of v4, /device:TPU:1, one launch (start us, length us, event | category | flops | bytes accessed | tf_op | source)
XLA Modules:
  0.0 90.3 jit_solution(17049043954034063503)
XLA Ops:
  0.6 87.4 %layer.1 = (bf16[3,96,8192]{2,1,0:T(8,128)(2,1)S(1)}, bf16[2,96,96]{2,1,0:T(8,128)(2,1)S(1)}, f32[2,96]{1,0:T(2,128)S(1)}) custom-call(bf16[96,96]{1,0:T(8,128)(2,1)} %tok_hbm.1, bf16[96,96]{1,0:T(8,128)(2,1)} %cot_hbm.1, s32[2,96]{1,0:T(2,128)} %bitcast.14, f32[2,96]{1,0:T(2,128)} %bitcast.15, bf16[3072,256]{1,0:T(8,128)(2,1)} %bitcast.11, ...), custom_call_target="tpu_custom_call" | custom-call | tf_op jit(solution)/shard_map/layer/pallas_call | solution.py:555
  88.0 2.2 %results.1 = (bf16[96,96]{1,0:T(8,128)(2,1)}, bf16[96,96]{1,0:T(8,128)(2,1)}, f32[2,96]{1,0:T(2,128)}, bf16[96,8192]{1,0:T(8,128)(2,1)}, bf16[96,8192]{1,0:T(8,128)(2,1)}, /*index=5*/bf16[96,8192]{1,0:T(8,128)(2,1)}) custom-call(bf16[3,96,8192]{2,1,0:T(8,128)(2,1)S(1)} %get-tuple-element.15.wide, bf16[2,96,96]{2,1,0:T(8,128)(2,1)S(1)} %get-tuple-element.16.rows, ...), custom_call_target="tpu_custom_call" | custom-call | tf_op jit(solution)/shard_map/results/pallas_call | solution.py:621

commit v5 on v4

--- a/solution.py
+++ b/solution.py
@@ -431,6 +431,11 @@
     partial(1 - g.c)
     cp.start("pair", part_ref.at[1 - g.c], sib, sib_dev)
     partial(g.c)
+    for d in dirs:
+        for h in (0, 1):
+            cp.wait(("p", h, d), act.at[h, spot(h, -d), g.c], nbr(h, 1, -d))
+            cp.start(("f", h, d), piece(h, -d, d), piece(h, -d, d), nbr(h, 1, d))
+            cross(h, -d)
     cp.wait("pair", sib, sib_dev)
 
     def add_pair(i, _):
@@ -461,11 +466,6 @@
             cp.wait(("r1", h, d), far.at[h, q], nbr(h, 2, -d))
             tmp[h, q] = (chip[share(h, d, q)].astype(F32) + far[h, q].astype(F32)).astype(BF16)
             cp.start(("r3", h, d), tmp.at[h, q], near.at[h, q, 0], nbr(h, 2, d))
-    for d in dirs:
-        for h in (0, 1):
-            cp.wait(("p", h, d), act.at[h, spot(h, -d), g.c], nbr(h, 1, -d))
-            cp.start(("f", h, d), piece(h, -d, d), piece(h, -d, d), nbr(h, 1, d))
-            cross(h, -d)
     for h in (0, 1):
         pass_on(h, 0)
     for d in dirs:

time: 90.4 us -> 89.8 us (level)
  no operation moved by 1% of the time
where the time goes in v5:
time: 89.8 us; the launch traced here: 89.7 us
  Pallas kernels  89.1 us (99%)
    pallas_call x1, Pallas kernels, layer(): pl.pallas_call(layer_kernel, out_shape=(pltpu.VMEM((3, width, n * size),...  86.9 us
    pallas_call x1, Pallas kernels, results(): pl.pallas_call(out_kernel, out_shape=tuple((jax.ShapeDtypeStruct(a, t) fo...  2.24 us

profile of v5, /device:TPU:1, one launch (start us, length us, event | category | flops | bytes accessed | tf_op | source)
XLA Modules:
  0.0 89.7 jit_solution(18395165557085875764)
XLA Ops:
  0.6 86.9 %layer.1 = (bf16[3,96,8192]{2,1,0:T(8,128)(2,1)S(1)}, bf16[2,96,96]{2,1,0:T(8,128)(2,1)S(1)}, f32[2,96]{1,0:T(2,128)S(1)}) custom-call(bf16[96,96]{1,0:T(8,128)(2,1)} %tok_hbm.1, bf16[96,96]{1,0:T(8,128)(2,1)} %cot_hbm.1, s32[2,96]{1,0:T(2,128)} %bitcast.14, f32[2,96]{1,0:T(2,128)} %bitcast.15, bf16[3072,256]{1,0:T(8,128)(2,1)} %bitcast.11, ...), custom_call_target="tpu_custom_call" | custom-call | tf_op jit(solution)/shard_map/layer/pallas_call | solution.py:555
  87.5 2.2 %results.1 = (bf16[96,96]{1,0:T(8,128)(2,1)}, bf16[96,96]{1,0:T(8,128)(2,1)}, f32[2,96]{1,0:T(2,128)}, bf16[96,8192]{1,0:T(8,128)(2,1)}, bf16[96,8192]{1,0:T(8,128)(2,1)}, /*index=5*/bf16[96,8192]{1,0:T(8,128)(2,1)}) custom-call(bf16[3,96,8192]{2,1,0:T(8,128)(2,1)S(1)} %get-tuple-element.15.wide, bf16[2,96,96]{2,1,0:T(8,128)(2,1)S(1)} %get-tuple-element.16.rows, ...), custom_call_target="tpu_custom_call" | custom-call | tf_op jit(solution)/shard_map/results/pallas_call | solution.py:621
